TPU v7x, 768 devices: a whole 4x8x12 slice. The times are simulated.
768 devices in a mesh: dp: 96 (over y, z_lo, core), mp: 8 (over z_hi, x).
Axes of the slice: x: 4, y: 8, z: 12 (z_hi: 2, z_lo: 6; z = z_hi * 6 + z_lo), core: 2. Of those that a mesh axis runs over, the one named last changes fastest.
Arguments:
- hidden_rows: bfloat16 [49152, 3584], P('dp'), may hold values from -6 to 6
- key_grad: bfloat16 [49152, 512], P('dp', 'mp'), may hold values from -6 to 6
- value_grad: bfloat16 [49152, 512], P('dp', 'mp'), may hold values from -6 to 6
- visual_rows: bfloat16 [24576, 1024], P('dp'), may hold values from -6 to 6
- visual_cotangent: bfloat16 [96, 4, 64, 3584], P('dp'), may hold values from -6 to 6
- norm_gain: float32 [1024], replicated, may hold values from 0.25 to 1.75
- norm_bias: float32 [1024], replicated, may hold values from -3 to 3
- fc1_weight: bfloat16 [1024, 4096], P(None, 'mp'), may hold values from -0.1875 to 0.1875
- fc1_bias: float32 [4096], P('mp'), may hold values from -3 to 3
- fc2_weight: bfloat16 [4096, 1024], P('mp'), may hold values from -0.09375 to 0.09375
- fc2_bias: float32 [1024], replicated, may hold values from -3 to 3
- layer_scale: float32 [1024], replicated, may hold values from 0.3 to 1.5
- token_counts: int32 [96, 8], P('dp'), may hold values from 1 to 32, as said below
- dest_offsets: int32 [96, 8], P('dp'), may hold values from 1 to 4, as said below
Outputs:
- key_weight_grad: float32 [3648, 512], P('dp', 'mp')
- value_weight_grad: float32 [3648, 512], P('dp', 'mp')
- projector_grad: float32 [3648, 1024], P('dp', 'mp')
- handoff: bfloat16 [96, 4, 64, 1024], P('dp', None, None, 'mp')
Inputs may be any that keep to these rules, and one draw needn't show every extreme that they name: `token_counts`: on every data rank the images of one distance, chosen per rank, all have 32 rows. `dest_offsets`: every data rank sends exactly 2 images to each distance from 1 to 4.
All inputs are finite; a program needn't handle non-finite values.
Results may differ from a plain program's by a relative error of at most 0.0046.
Values may be sent and summed in bfloat16 or wider, within the bound.
A program may use at most 64 MiB of HBM per device.

v0:
```python
import jax
import jax.numpy as jnp
from jax import lax
from jax.sharding import PartitionSpec as P

SPREAD = 4
CAP = 64


def in_blocks(x, dim, count):
    shape = x.shape
    parts = x.reshape(*shape[:dim], count, shape[dim] // count, *shape[dim + 1 :])
    return jnp.moveaxis(parts, dim, 0)


def sent_and_summed(x, axis, dim):
    count = lax.axis_size(axis)
    parts = lax.all_to_all(in_blocks(x, dim, count), axis, 0, 0, tiled=True)
    return jnp.sum(parts, axis=0)


def shifted(x, axis, by):
    count = lax.axis_size(axis)
    return lax.ppermute(x, axis, [(i, (i + by) % count) for i in range(count)])


def own_tiles(x, axis, dim):
    count = lax.axis_size(axis)
    parts = in_blocks(x, dim, count)
    lines = parts.reshape(count, -1)
    extent = max(16, -(-lines.shape[1] // 1024) * 8)
    lines = jnp.pad(lines, ((0, 0), (0, extent * 128 - lines.shape[1]))).reshape(-1, 128)
    own = lax.psum_scatter(lines, axis, scatter_dimension=0, tiled=True)
    return own.reshape(-1)[: parts[0].size].reshape(parts.shape[1:])


def pack_rows(rows, counts, offsets):
    total_rows = rows.shape[0]
    images = counts.shape[0]
    ends = jnp.cumsum(counts)
    starts = ends - counts
    places = jnp.arange(total_rows)
    image_ids = jnp.arange(images)
    owner = jnp.sum((places[:, None] >= ends[None, :]).astype(jnp.int32), axis=1)
    member = (owner[:, None] == image_ids[None, :]).astype(jnp.int32)
    earlier = (image_ids[None, :] < image_ids[:, None]) & (offsets[None, :] == offsets[:, None])
    before = jnp.sum(earlier.astype(jnp.int32) * counts[None, :], axis=1)
    row_dest = jnp.sum(member * offsets[None, :], axis=1)
    row_start = jnp.sum(member * starts[None, :], axis=1)
    row_before = jnp.sum(member * before[None, :], axis=1)
    slot_index = row_before + places - row_start
    target = jnp.where(places < ends[images - 1], (row_dest - 1) * CAP + slot_index, -1)
    slot_ids = jnp.arange(SPREAD * CAP)
    select = (slot_ids[:, None] == target[None, :]).astype(jnp.bfloat16)
    packed = jnp.dot(select, rows, preferred_element_type=jnp.float32).astype(jnp.bfloat16)
    return packed.reshape(SPREAD, CAP, rows.shape[1])


def vision(
    visual_rows,
    norm_gain,
    norm_bias,
    fc1_weight,
    fc1_bias,
    fc2_weight,
    fc2_bias,
    layer_scale,
    token_counts,
    dest_offsets,
):
    values = visual_rows.astype(jnp.float32)
    center = jnp.mean(values, axis=1, keepdims=True)
    spread_sq = jnp.mean((values - center) ** 2, axis=1, keepdims=True)
    normed = ((values - center) * lax.rsqrt(spread_sq + 1e-06) * norm_gain + norm_bias).astype(
        jnp.bfloat16
    )
    hidden = jax.nn.gelu(
        jnp.dot(normed, fc1_weight, preferred_element_type=jnp.float32) + fc1_bias,
        approximate=False,
    ).astype(jnp.bfloat16)
    partial_value = jnp.dot(hidden, fc2_weight, preferred_element_type=jnp.float32)
    summed = sent_and_summed(partial_value, "mp", 1)
    column_count = summed.shape[1]
    first_col = lax.axis_index("mp") * column_count
    own_values = lax.dynamic_slice_in_dim(values, first_col, column_count, 1)
    own_scale = lax.dynamic_slice_in_dim(layer_scale, first_col, column_count, 0)
    own_bias = lax.dynamic_slice_in_dim(fc2_bias, first_col, column_count, 0)
    encoded = (own_values + own_scale * (summed + own_bias)).astype(jnp.bfloat16)
    packed = pack_rows(encoded, token_counts[0], dest_offsets[0])
    received = []
    for distance in range(SPREAD):
        received.append(shifted(packed[distance], "dp", distance + 1))
    return jnp.stack(received, axis=0)[None]


def per_device(
    hidden_rows,
    key_grad,
    value_grad,
    visual_rows,
    visual_cotangent,
    norm_gain,
    norm_bias,
    fc1_weight,
    fc1_bias,
    fc2_weight,
    fc2_bias,
    layer_scale,
    token_counts,
    dest_offsets,
):
    tokens_here, width = hidden_rows.shape
    devices = lax.axis_size("dp")
    shard_rows = (width + devices) // devices
    padded_width = shard_rows * devices
    ones_column = jnp.ones((tokens_here, 1), jnp.bfloat16)
    zero_columns = jnp.zeros((tokens_here, padded_width - width - 1), jnp.bfloat16)
    augmented = jnp.concatenate([hidden_rows, ones_column, zero_columns], axis=1)
    key_cols = key_grad.shape[1]
    kv_cotangent = jnp.concatenate([key_grad, value_grad], axis=1)

    def make_projector(handoff):
        slot_count = handoff.shape[1] * handoff.shape[2]
        cot_flat = visual_cotangent.reshape(slot_count, width)
        cot_padded = jnp.concatenate(
            [cot_flat, jnp.zeros((slot_count, padded_width - width), jnp.bfloat16)], axis=1
        )
        received_rows = handoff.reshape(slot_count, handoff.shape[3])

        def projector_rows(start, count):
            return lax.dot_general(
                cot_padded,
                received_rows,
                (((0,), (0,)), ((), ())),
                preferred_element_type=jnp.float32,
            )

        return projector_rows

    handoff = vision(
        visual_rows,
        norm_gain,
        norm_bias,
        fc1_weight,
        fc1_bias,
        fc2_weight,
        fc2_bias,
        layer_scale,
        token_counts,
        dest_offsets,
    )
    projector_rows = make_projector(handoff)
    results = own_tiles(
        jnp.concatenate(
            [
                lax.dot_general(
                    augmented,
                    kv_cotangent,
                    (((0,), (0,)), ((), ())),
                    preferred_element_type=jnp.float32,
                ),
                projector_rows(jnp.int32(0), shard_rows * lax.axis_size("dp")),
            ],
            axis=1,
        ),
        "dp",
        0,
    )
    key_weight_grad = results[:, :key_cols]
    value_weight_grad = results[:, key_cols : 2 * key_cols]
    projector_grad = results[:, 2 * key_cols :]
    return (key_weight_grad, value_weight_grad, projector_grad, handoff)


def solution(mesh):
    placed = (
        P("dp", None),
        P("dp", "mp"),
        P("dp", "mp"),
        P("dp", None),
        P("dp", None, None, None),
        P(),
        P(),
        P(None, "mp"),
        P("mp"),
        P("mp", None),
        P(),
        P(),
        P("dp", None),
        P("dp", None),
    )
    return jax.shard_map(
        per_device,
        mesh=mesh,
        in_specs=placed,
        out_specs=(P("dp", "mp"), P("dp", "mp"), P("dp", "mp"), P("dp", None, None, "mp")),
        check_vma=False,
    )
```

profile of v0, /device:TPU:1, one launch (start us, length us, event | category | flops | bytes accessed | tf_op | source)
XLA Modules:
  0.0 684.7 jit_solution(11277988769444244215)
XLA Ops:
  7.2 0.0 copy-start
  7.2 1.3 convert_reduce_fusion
  8.5 1.3 multiply_reduce_fusion
  9.8 0.0 copy-done
  9.8 3.3 convolution_bitcast_fusion
  13.2 0.0 copy-start.1
  13.2 0.0 copy-start.6
  13.2 1.1 copy.22
  14.2 17.5 %all-to-all-start = ((f32[8,256,128]{2,1,0:T(8,128)}), f32[8,256,128]{2,1,0:T(8,128)S(1)}, u32[]{:S(2)}, u32[]{:S(2)}) async-start(f32[8,256,128]{2,1,0:T(8,128)} %bitcast.32), calls=%async_computation | async-start | bytes 2097152 | tf_op jit(solution)/shard_map/all_to_all | solution.py:18
  31.7 0.0 reduce-scatter.2.cloned.1.call-start
  31.8 0.0 copy-done.1
  31.8 1.1 convert_element_type.24
  32.9 0.2 reduce-window.4
  33.1 0.6 slice.33
  33.7 0.8 dynamic_slice.11
  34.5 0.8 dynamic_slice.10
  35.3 0.0 copy-start.5
  35.3 0.0 copy-start.3
  35.3 0.0 copy-start.4
  35.3 6.6 concatenate.12
  41.9 0.1 convert_reduce_fusion.1
  42.0 0.2 select_reduce_fusion.3
  42.2 0.1 select_reduce_fusion.2
  42.3 0.7 compare_select_fusion
  42.9 8.6 %all-to-all-done = f32[8,256,128]{2,1,0:T(8,128)S(1)} async-done(((f32[8,256,128]{2,1,0:T(8,128)}), f32[8,256,128]{2,1,0:T(8,128)S(1)}, u32[]{:S(2)}, u32[]{:S(2)}) %all-to-all-start) | async-done | bytes 1048608 | tf_op jit(solution)/shard_map/all_to_all | solution.py:18
  51.5 0.1 reduce_sum.79
  51.6 1.1 convolution_convert_fusion
  52.7 27.2 %collective-permute-start = (bf16[64,128]{1,0:T(8,128)(2,1)S(1)}, bf16[64,128]{1,0:T(8,128)(2,1)S(1)}, u32[]{:S(2)}, u32[]{:S(2)}) collective-permute-start(bf16[64,128]{1,0:T(8,128)(2,1)S(1)} %get-tuple-element.9), channel_id=1, source_target_pairs={{0,8},{8,16},{16,24},{24,32},{32,40},{40,48},{48,56},{56,64},{64,7... | collective-permute-start | bytes 49160 | tf_op jit(solution)/shard_map/ppermute | solution.py:24
  79.9 1.9 collective-permute-start.3
  81.8 5.2 collective-permute-start.2
  87.1 0.0 copy-start.2
  87.1 2.1 collective-permute-start.1
  89.2 3.2 fusion.47
  92.4 0.0 collective-permute-done
  92.4 0.0 collective-permute-done.3
  92.4 1.4 collective-permute-done.2
  93.8 4.8 collective-permute-done.1
  98.6 0.6 fusion.89
  99.3 0.7 fusion
  99.9 2.1 pad_maximum_fusion
  102.0 5.3 reshape_reshape.3
  107.3 4.3 pad.5
  111.7 5.1 reshape.85
  116.7 0.0 reduce-scatter.2.cloned.1.call-update
  116.8 559.0 %reduce-scatter.2.cloned.1.call-done = f32[80,128]{1,0:T(8,128)} async-done(((f32[7680,128]{1,0:T(8,128)}), f32[80,128]{1,0:T(8,128)}) %reduce-scatter.2.cloned.1.call-update) | async-done | bytes 40976 | tf_op jit(solution)/shard_map/reduce_scatter | solution.py:33
  675.7 0.8 reshape.86
  676.5 0.6 slice.49
  677.1 0.7 fusion.91
  (11 shorter events, 0.1 us)
Async XLA Ops:
  7.2 2.6 copy-start
  13.2 18.6 %copy-start.1 = (bf16[256,1024]{1,0:T(8,128)(2,1)S(1)}, bf16[256,1024]{1,0:T(8,128)(2,1)}, u32[]{:S(2)}) copy-start(bf16[256,1024]{1,0:T(8,128)(2,1)} %param.17) | copy-start | bytes 1572868
  13.2 19.8 %copy-start.6 = (s32[1,8]{1,0:T(1,128)S(1)}, s32[1,8]{1,0:T(1,128)}, u32[]{:S(2)}) copy-start(s32[1,8]{1,0:T(1,128)} %param.26) | copy-start | bytes 100
  14.2 37.3 %all-to-all-start = ((f32[8,256,128]{2,1,0:T(8,128)}), f32[8,256,128]{2,1,0:T(8,128)S(1)}, u32[]{:S(2)}, u32[]{:S(2)}) async-start(f32[8,256,128]{2,1,0:T(8,128)} %bitcast.32), calls=%async_computation | async-start | bytes 2097152 | tf_op jit(solution)/shard_map/all_to_all | solution.py:18
  31.7 644.0 %reduce-scatter.2.cloned.1.call-start = ((), (), s32[]{:S(2)}) async-start(), calls=%async_computation.2 | async-start | bytes 3973120 | tf_op jit(solution)/shard_map/reduce_scatter | solution.py:33
  35.3 6.7 copy-start.5
  35.3 53.9 %copy-start.3 = (bf16[512,64]{0,1:T(8,128)(2,1)S(1)}, bf16[512,64]{0,1:T(8,128)(2,1)}, u32[]{:S(2)}) copy-start(bf16[512,64]{0,1:T(8,128)(2,1)} %param.16) | copy-start | bytes 196612
  35.3 53.9 %copy-start.4 = (bf16[512,64]{0,1:T(8,128)(2,1)S(1)}, bf16[512,64]{0,1:T(8,128)(2,1)}, u32[]{:S(2)}) copy-start(bf16[512,64]{0,1:T(8,128)(2,1)} %param.15) | copy-start | bytes 196612
  52.7 39.7 %collective-permute-start = (bf16[64,128]{1,0:T(8,128)(2,1)S(1)}, bf16[64,128]{1,0:T(8,128)(2,1)S(1)}, u32[]{:S(2)}, u32[]{:S(2)}) collective-permute-start(bf16[64,128]{1,0:T(8,128)(2,1)S(1)} %get-tuple-element.9), channel_id=1, source_target_pairs={{0,8},{8,16},{16,24},{24,32},{32,40},{40,48},{48,56},{56,64},{64,7... | collective-permute-start | bytes 49160 | tf_op jit(solution)/shard_map/ppermute | solution.py:24
  79.9 12.5 %collective-permute-start.3 = (bf16[64,128]{1,0:T(8,128)(2,1)S(1)}, bf16[64,128]{1,0:T(8,128)(2,1)S(1)}, u32[]{:S(2)}, u32[]{:S(2)}) collective-permute-start(bf16[64,128]{1,0:T(8,128)(2,1)S(1)} %get-tuple-element.10), channel_id=1, source_target_pairs={{0,32},{8,40},{16,48},{24,56},{32,64},{40,72},{48,80},{56,88},{64,... | collective-permute-start | bytes 49160 | tf_op jit(solution)/shard_map/ppermute | solution.py:24
  81.8 12.0 %collective-permute-start.2 = (bf16[64,128]{1,0:T(8,128)(2,1)S(1)}, bf16[64,128]{1,0:T(8,128)(2,1)S(1)}, u32[]{:S(2)}, u32[]{:S(2)}) collective-permute-start(bf16[64,128]{1,0:T(8,128)(2,1)S(1)} %get-tuple-element.11), channel_id=1, source_target_pairs={{0,24},{8,32},{16,40},{24,48},{32,56},{40,64},{48,72},{56,80},{64,... | collective-permute-start | bytes 49160 | tf_op jit(solution)/shard_map/ppermute | solution.py:24
  87.1 12.2 %copy-start.2 = (bf16[1,4,64,3584]{3,2,1,0:T(8,128)(2,1)S(1)}, bf16[1,4,64,3584]{3,2,1,0:T(8,128)(2,1)}, u32[]{:S(2)}) copy-start(bf16[1,4,64,3584]{3,2,1,0:T(8,128)(2,1)} %param.18) | copy-start | bytes 5505028
  87.1 11.5 %collective-permute-start.1 = (bf16[64,128]{1,0:T(8,128)(2,1)S(1)}, bf16[64,128]{1,0:T(8,128)(2,1)S(1)}, u32[]{:S(2)}, u32[]{:S(2)}) collective-permute-start(bf16[64,128]{1,0:T(8,128)(2,1)S(1)} %get-tuple-element.12), channel_id=1, source_target_pairs={{0,16},{8,24},{16,32},{24,40},{32,48},{40,56},{48,64},{56,72},{64,... | collective-permute-start | bytes 49160 | tf_op jit(solution)/shard_map/ppermute | solution.py:24
Sparse Core Ops, SparseCore 0:
  116.9 558.8 reduce-scatter.1
where the time goes:
time: 692 us; the launch traced here: 685 us
  waiting for transfers between devices  574 us (83%)
  starting transfers between devices  53.9 us (8%)
  local copies, waits for them, and re-layouts  26.7 us (4%)
  between operations  14.2 us (2%)
  matrix products  8.35 us (1%)
  other arithmetic  7.68 us (1%)
    reduce_scatter x1, waiting for transfers between devices, own_tiles(): own = lax.psum_scatter(lines, axis, scatter_dimension=0, tiled=True)  559 us
    ppermute x4, starting transfers between devices, shifted(): return lax.ppermute(x, axis, [(i, (i + by) % count) for i in range(count)])  36.4 us
    all_to_all x1, starting transfers between devices, sent_and_summed(): parts = lax.all_to_all(in_blocks(x, dim, count), axis, 0, 0, tiled=True)  17.5 us
  transfers between devices with their start and end apart: 6, of which 4 were waited for; matrix products, arithmetic and copies ran while one was open for 2% of the time, Pallas kernels for 0%

commit v1 on v0

v1 whole, which is shorter than its diff:
```python
import functools

import jax
import jax.numpy as jnp
from jax import lax
from jax.experimental import pallas as pl
from jax.experimental.pallas import tpu as pltpu
from jax.sharding import PartitionSpec as P

MESH = pl.DeviceIdType.MESH
F32 = jnp.float32
BF16 = jnp.bfloat16

NX, NY, NZ, NCORE, NHALF = 4, 8, 6, 2, 2
N_DP = NY * NZ * NCORE
SPREAD, CAP = 4, 64
SLOTS = SPREAD * CAP
IMAGES = 8
OWN = 38
BLK = 40
YROWS = NZ * NCORE * OWN


def kernel(
    hid_hbm, kg_hbm, vg_hbm, vis_hbm, cot_hbm, gain_hbm, nb_hbm, w1_hbm, b1_hbm, w2_hbm, b2_hbm, ls_hbm,
    cnt_ref, off_ref,
    key_o, val_o, proj_o, hand_o,
    hid, kg, vg, vis, cot, gain, nb, w1, b1, w2, b2, ls,
    packed, part, xs, xr, vs, vr, hs, hr, hand, hpar,
    kvf, kvo, kvp, cotf, amat, apar,
    s1, r1y, r1z, s2, r2, keyv, valv, projv,
    lsem, osem, dsem_s, dsem_r, xsem_s, xsem_r, vsem_s, vsem_r, hsem_s, hsem_r,
    y_s, y_r, z_s, z_r,
):
    dp = lax.axis_index("dp")
    mp = lax.axis_index("mp")
    core = lax.rem(dp, 2)
    zlo = lax.rem(lax.div(dp, 2), NZ)
    y = lax.div(dp, NZ * NCORE)
    zhi = lax.div(mp, NX)
    x = lax.rem(mp, NX)
    partner = (dp + 1 - 2 * core, mp)

    def rank_of(y_, z_):
        return (y_ * NZ + z_) * NCORE + core

    loads = [
        (vis_hbm, vis), (w1_hbm, w1), (gain_hbm, gain), (nb_hbm, nb), (b1_hbm, b1), (w2_hbm, w2),
        (b2_hbm, b2), (ls_hbm, ls), (kg_hbm, kg), (vg_hbm, vg), (hid_hbm, hid), (cot_hbm.at[0], cot),
    ]
    copies = [pltpu.make_async_copy(s, d, lsem.at[i]) for i, (s, d) in enumerate(loads)]
    for c in copies:
        c.start()
    (l_vis, l_w1, l_gain, l_nb, l_b1, l_w2, l_b2, l_ls, l_kg, l_vg, l_hid, l_cot) = copies

    barrier = pltpu.get_barrier_semaphore()
    greeted = [partner]
    greeted += [(rank_of(lax.rem(y + d, NY), zlo), mp) for d in range(1, NY)]
    greeted += [(rank_of(y, lax.rem(zlo + d, NZ)), mp) for d in range(1, NZ)]
    greeted += [(dp, zhi * NX + lax.rem(x + d, NX)) for d in range(1, NX)]
    for k in range(1, SPREAD + 1):
        for e in range(NHALF):
            greeted.append((lax.rem(dp + k, N_DP), e * NX + x))
            greeted.append((lax.rem(dp + N_DP - k, N_DP), e * NX + x))
    for who in greeted:
        pl.semaphore_signal(barrier, 1, device_id=who, device_id_type=MESH)

    place = lax.broadcasted_iota(jnp.int32, (1, SLOTS), 1)
    target = jnp.full((1, SLOTS), -1, jnp.int32)
    counts = [cnt_ref[0, i] for i in range(IMAGES)]
    offs = [off_ref[0, i] for i in range(IMAGES)]
    start = jnp.int32(0)
    for i in range(IMAGES):
        end = start + counts[i]
        before = jnp.int32(0)
        for j in range(i):
            before = before + jnp.where(offs[j] == offs[i], counts[j], 0)
        base = (offs[i] - 1) * CAP + before - start
        inside = (place >= start) & (place < end)
        target = jnp.where(inside, place + base, target)
        start = end
    filled = []
    for k in range(1, SPREAD + 1):
        total = jnp.int32(0)
        for i in range(IMAGES):
            total = total + jnp.where(offs[i] == k, counts[i], 0)
        filled.append(total)
    slot_ids = lax.broadcasted_iota(jnp.int32, (SLOTS, SLOTS), 0)
    select = jnp.where(slot_ids == target, 1.0, 0.0).astype(BF16)

    l_vis.wait()
    packed[...] = jnp.dot(select, vis[...], preferred_element_type=F32).astype(BF16)
    values = packed[...].astype(F32)
    center = jnp.mean(values, axis=1, keepdims=True)
    delta = values - center
    spread_sq = jnp.mean(delta * delta, axis=1, keepdims=True)
    l_gain.wait()
    l_nb.wait()
    normed = (delta * lax.rsqrt(spread_sq + 1e-06) * gain[...] + nb[...]).astype(BF16)
    l_w1.wait()
    l_b1.wait()
    pre = jnp.dot(normed, w1[...], preferred_element_type=F32) + b1[...]
    hidden = (0.5 * pre * (1.0 + lax.erf(pre * (0.5**0.5)))).astype(BF16)
    l_w2.wait()
    part[...] = jnp.dot(hidden, w2[...], preferred_element_type=F32)
    for xd in range(NX):
        for e in range(NHALF):
            cols = (e * NX + xd) * 128
            for k in range(SPREAD):
                xs[xd, k, e] = part[k * CAP : (k + 1) * CAP, cols : cols + 128].astype(BF16)

    pl.semaphore_wait(barrier, len(greeted))

    def x_copy(d, k):
        return pltpu.make_async_remote_copy(
            src_ref=xs.at[lax.rem(x + d, NX), k], dst_ref=xr.at[d - 1, k],
            send_sem=xsem_s.at[d - 1, k], recv_sem=xsem_r.at[d - 1, k],
            device_id=(dp, zhi * NX + lax.rem(x + d, NX)), device_id_type=MESH,
        )

    for k in range(SPREAD):
        for d in (2, 1, 3):
            x_copy(d, k).start()

    def v_copy(k):
        return pltpu.make_async_remote_copy(
            src_ref=vs.at[k], dst_ref=vr.at[k], send_sem=vsem_s.at[k], recv_sem=vsem_r.at[k],
            device_id=(lax.rem(dp + k + 1, N_DP), mp), device_id_type=MESH,
        )

    own_cols = pl.ds(pl.multiple_of(mp * 128, 128), 128)
    for k in range(SPREAD):
        vs[k] = packed[k * CAP : (k + 1) * CAP, own_cols]
        v_copy(k).start()

    l_kg.wait()
    l_vg.wait()
    l_hid.wait()
    kv = jnp.concatenate([kg[...], vg[...]], axis=1)

    @pl.loop(0, 7)
    def _(i):
        cols = pl.ds(pl.multiple_of(i * 512, 512), 512)
        kvf[cols, :] = lax.dot_general(
            hid[:, cols], kv, (((0,), (0,)), ((), ())), preferred_element_type=F32
        )

    colsum = jnp.sum(kv.astype(F32), axis=0, keepdims=True)
    tail_row = lax.broadcasted_iota(jnp.int32, (80, 128), 0)
    kvf[3584:3664, :] = jnp.where(tail_row == 0, colsum, 0.0)

    @pl.loop(0, NY)
    def _(yy):
        win = kvf[pl.ds(pl.multiple_of(yy * YROWS, 8), YROWS + 8), :]
        for z in range(NZ):
            for c in range(NCORE):
                at = (z * NCORE + c) * OWN
                kvo[c, yy, z] = win[at : at + BLK, :]

    def d_copy(src, dst, i):
        return pltpu.make_async_remote_copy(
            src_ref=src, dst_ref=dst, send_sem=dsem_s.at[i], recv_sem=dsem_r.at[i],
            device_id=partner, device_id_type=MESH,
        )

    kv_swap = d_copy(kvo.at[1 - core], kvp, 0)
    kv_swap.start()

    def y_copy(g, d):
        to = lax.rem(y + d, NY)
        return pltpu.make_async_remote_copy(
            src_ref=s1.at[g, to], dst_ref=r1y.at[g, d - 1],
            send_sem=y_s.at[g, d - 1], recv_sem=y_r.at[g, d - 1],
            device_id=(rank_of(to, zlo), mp), device_id_type=MESH,
        )

    def z_copy(g, d):
        to = lax.rem(zlo + d, NZ)
        return pltpu.make_async_remote_copy(
            src_ref=s2.at[g, to], dst_ref=r2.at[g, d - 1],
            send_sem=z_s.at[g, d - 1], recv_sem=z_r.at[g, d - 1],
            device_id=(rank_of(y, to), mp), device_id_type=MESH,
        )

    kv_swap.wait()

    @pl.loop(0, NY)
    def _(yy):
        s1[0, yy] = (kvo[core, yy] + kvp[yy]).astype(BF16)

    for d in (4, 3, 5, 2, 6, 1, 7):
        y_copy(0, d).start()

    def h_copy(e, k):
        return pltpu.make_async_remote_copy(
            src_ref=hs.at[e, k], dst_ref=hr.at[zhi, k], send_sem=hsem_s.at[e, k], recv_sem=hsem_r.at[zhi, k],
            device_id=(lax.rem(dp + k + 1, N_DP), e * NX + x), device_id_type=MESH,
        )

    def h_wait(e, k):
        pltpu.make_async_remote_copy(
            src_ref=hs.at[e, k], dst_ref=hr.at[e, k], send_sem=hsem_s.at[e, k], recv_sem=hsem_r.at[e, k],
            device_id=(lax.rem(dp + k + 1, N_DP), e * NX + x), device_id_type=MESH,
        ).wait_recv()

    l_b2.wait()
    l_ls.wait()
    with_bias = jnp.where(zhi == 0, 1.0, 0.0)
    slot_in = lax.broadcasted_iota(jnp.int32, (CAP, 128), 0)
    for k in range(SPREAD):
        for d in range(1, NX):
            x_copy(d, k).wait_recv()
        for e in range(NHALF):
            cols = pl.ds(pl.multiple_of((e * NX + x) * 128, 128), 128)
            total = part[k * CAP : (k + 1) * CAP, cols]
            for d in range(1, NX):
                total = total + xr[d - 1, k, e].astype(F32)
            branch = ls[:, cols] * (total + with_bias * b2[:, cols])
            hs[e, k] = jnp.where(slot_in < filled[k], branch, 0.0).astype(BF16)
            h_copy(e, k).start()

    l_cot.wait()

    @pl.loop(0, 28)
    def _(i):
        cols = pl.ds(pl.multiple_of(i * 128, 128), 128)
        block = cot[:, :, cols].reshape(SLOTS, 128).astype(F32)
        cotf[cols, :] = block.T

    cotf[3584:3664, :] = jnp.zeros((80, SLOTS), F32)

    @pl.loop(0, NY)
    def _(yy):
        win = cotf[pl.ds(pl.multiple_of(yy * YROWS, 8), YROWS + 8), :]
        for c in range(NCORE):
            rows = [win[(z * NCORE + c) * OWN : (z * NCORE + c) * OWN + BLK, :] for z in range(NZ)]
            amat[c, yy] = jnp.concatenate(rows, axis=0).astype(BF16)

    a_swap = d_copy(amat.at[1 - core], apar, 1)
    a_swap.start()

    for k in range(SPREAD):
        v_copy(k).wait_recv()
        for e in range(NHALF):
            h_wait(e, k)
        hand[k] = (vr[k].astype(F32) + (hr[0, k].astype(F32) + hr[1, k].astype(F32))).astype(BF16)
    h_swap = d_copy(hand, hpar, 2)
    h_swap.start()
    out_hand = pltpu.make_async_copy(hand, hand_o.at[0], osem.at[0])
    out_hand.start()
    a_swap.wait()
    h_swap.wait()
    mine = hand[...].reshape(SLOTS, 128)
    theirs = hpar[...].reshape(SLOTS, 128)

    @pl.loop(0, NY)
    def _(yy):
        res = jnp.dot(amat[core, yy], mine, preferred_element_type=F32)
        res = res + jnp.dot(apar[yy], theirs, preferred_element_type=F32)
        for z in range(NZ):
            s1[1, yy, z] = res[z * BLK : (z + 1) * BLK, :].astype(BF16)

    for d in (4, 3, 5, 2, 6, 1, 7):
        y_copy(1, d).start()

    for g in range(2):
        total = s1[g, y].astype(F32)
        for d in range(1, NY):
            y_copy(g, d).wait_recv()
            total = total + r1y[g, d - 1].astype(F32)
        s2[g] = total.astype(BF16)
        for d in (5, 4, 3, 2, 1):
            z_copy(g, d).start()
    for g in range(2):
        total = s2[g, zlo].astype(F32)
        for d in range(1, NZ):
            z_copy(g, d).wait_recv()
            total = total + r2[g, d - 1].astype(F32)
        if g == 0:
            keyv[...] = total[:OWN, :64]
            valv[...] = total[:OWN, 64:]
            out_key = pltpu.make_async_copy(keyv, key_o, osem.at[1])
            out_val = pltpu.make_async_copy(valv, val_o, osem.at[2])
            out_key.start()
            out_val.start()
        else:
            projv[...] = total[:OWN, :]
            out_proj = pltpu.make_async_copy(projv, proj_o, osem.at[3])
            out_proj.start()

    for k in range(SPREAD):
        for d in range(1, NX):
            x_copy(d, k).wait_send()
        v_copy(k).wait_send()
        for e in range(NHALF):
            h_copy(e, k).wait_send()
    for g in range(2):
        for d in range(1, NY):
            y_copy(g, d).wait_send()
        for d in range(1, NZ):
            z_copy(g, d).wait_send()
    out_hand.wait()
    out_key.wait()
    out_val.wait()
    out_proj.wait()


def per_device(
    hidden_rows, key_grad, value_grad, visual_rows, visual_cotangent, norm_gain, norm_bias,
    fc1_weight, fc1_bias, fc2_weight, fc2_bias, layer_scale, token_counts, dest_offsets,
):
    anyspec = pl.BlockSpec(memory_space=pl.ANY)
    smem = pl.BlockSpec(memory_space=pltpu.SMEM)
    dma = pltpu.SemaphoreType.DMA
    V = pltpu.VMEM
    scratch = [
        V((512, 3584), BF16), V((512, 64), BF16), V((512, 64), BF16), V((256, 1024), BF16),
        V((4, 64, 3584), BF16), V((1, 1024), F32), V((1, 1024), F32), V((1024, 512), BF16), V((1, 512), F32),
        V((512, 1024), BF16), V((1, 1024), F32), V((1, 1024), F32),
        V((256, 1024), BF16), V((256, 1024), F32),
        V((NX, SPREAD, NHALF, CAP, 128), BF16), V((NX - 1, SPREAD, NHALF, CAP, 128), BF16),
        V((SPREAD, CAP, 128), BF16), V((SPREAD, CAP, 128), BF16),
        V((NHALF, SPREAD, CAP, 128), BF16), V((NHALF, SPREAD, CAP, 128), BF16),
        V((SPREAD, CAP, 128), BF16), V((SPREAD, CAP, 128), BF16),
        V((3664, 128), F32), V((NCORE, NY, NZ, BLK, 128), F32), V((NY, NZ, BLK, 128), F32),
        V((3664, 256), F32), V((NCORE, NY, NZ * BLK, 256), BF16), V((NY, NZ * BLK, 256), BF16),
        V((2, NY, NZ, BLK, 128), BF16), V((2, NY - 1, NZ, BLK, 128), BF16), V((8, 128), F32),
        V((2, NZ, BLK, 128), BF16), V((2, NZ - 1, BLK, 128), BF16),
        V((OWN, 64), F32), V((OWN, 64), F32), V((OWN, 128), F32),
        dma((12,)), dma((4,)), dma((3,)), dma((3,)),
        dma((NX - 1, SPREAD)), dma((NX - 1, SPREAD)), dma((SPREAD,)), dma((SPREAD,)),
        dma((NHALF, SPREAD)), dma((NHALF, SPREAD)),
        dma((2, NY - 1)), dma((2, NY - 1)), dma((2, NZ - 1)), dma((2, NZ - 1)),
    ]
    key_g, value_g, proj_g, handoff = pl.pallas_call(
        kernel,
        out_shape=(
            jax.ShapeDtypeStruct((OWN, 64), F32),
            jax.ShapeDtypeStruct((OWN, 64), F32),
            jax.ShapeDtypeStruct((OWN, 128), F32),
            jax.ShapeDtypeStruct((1, SPREAD, CAP, 128), BF16),
        ),
        in_specs=[anyspec] * 12 + [smem] * 2,
        out_specs=[anyspec] * 4,
        scratch_shapes=scratch,
        compiler_params=pltpu.CompilerParams(
            collective_id=0, has_side_effects=True, vmem_limit_bytes=60 * 1024 * 1024
        ),
        name="bucket",
    )(
        hidden_rows, key_grad, value_grad, visual_rows, visual_cotangent,
        norm_gain.reshape(1, -1), norm_bias.reshape(1, -1), fc1_weight, fc1_bias.reshape(1, -1),
        fc2_weight, fc2_bias.reshape(1, -1), layer_scale.reshape(1, -1), token_counts, dest_offsets,
    )
    return key_g, value_g, proj_g, handoff


def solution(mesh):
    placed = (
        P("dp", None), P("dp", "mp"), P("dp", "mp"), P("dp", None), P("dp", None, None, None),
        P(), P(), P(None, "mp"), P("mp"), P("mp", None), P(), P(), P("dp", None), P("dp", None),
    )
    return jax.shard_map(
        per_device,
        mesh=mesh,
        in_specs=placed,
        out_specs=(P("dp", "mp"), P("dp", "mp"), P("dp", "mp"), P("dp", None, None, "mp")),
        check_vma=False,
    )
```

time: 692 us -> 65.3 us (0.09)
  waiting for transfers between devices: 574 us -> 0 us
  Pallas kernels: 0 us -> 55.6 us
  starting transfers between devices: 53.9 us -> 0 us
  local copies, waits for them, and re-layouts: 26.7 us -> 8.66 us
  between operations: 14.2 us -> 0.64 us
  matrix products: 8.35 us -> 0 us
  other arithmetic: 7.68 us -> 0 us
    reduce_scatter x1 -> x0, waiting for transfers between devices: 559 us -> none  [own_tiles(): own = lax.psum_scatter(lines, axis, scatter_dimension=0, tiled=True)]
    pallas_call x0 -> x1, Pallas kernels: none -> 55.6 us  [per_device(): pl.pallas_call(kernel, out_shape=(jax.ShapeDtypeStruct((OWN, 64), F32), j...]
    ppermute x4 -> x0, starting transfers between devices: 36.4 us -> none  [shifted(): return lax.ppermute(x, axis, [(i, (i + by) % count) for i in range(count)])]
    all_to_all x1 -> x0, starting transfers between devices: 17.5 us -> none  [sent_and_summed(): parts = lax.all_to_all(in_blocks(x, dim, count), axis, 0, 0, tiled=True)]
    unnamed x14 -> x6, local copies, waits for them, and re-layouts: 0.05 us -> 8.66 us
    all_to_all x1 -> x0, waiting for transfers between devices: 8.6 us -> none  [sent_and_summed(): parts = lax.all_to_all(in_blocks(x, dim, count), axis, 0, 0, tiled=True)]
    dot_general x4 -> x0, matrix products: 8.35 us -> none  [the longest x1 3.34 us: vision(): jnp.dot(hidden, fc2_weight, preferred_element_type=jnp.float32)]
    reshape x3 -> x0, local copies, waits for them, and re-layouts: 6.94 us -> none  [the longest x1 5.08 us: own_tiles(): jnp.pad(lines, ((0, 0), (0, extent * 128 - lines.shape[1])))]
  transfers between devices with their start and end apart: 6 -> 0, of which waited for: 4 -> 0; matrix products, arithmetic and copies ran while one was open for 2% -> 0% of each run, Pallas kernels for 0% -> 0%
where the time goes in v1:
time: 65.3 us; the launch traced here: 64.9 us
  Pallas kernels  55.6 us (85%)
  local copies, waits for them, and re-layouts  8.66 us (13%)
    pallas_call x1, Pallas kernels, per_device(): pl.pallas_call(kernel, out_shape=(jax.ShapeDtypeStruct((OWN, 64), F32), j...  55.6 us
    unnamed x6, local copies, waits for them, and re-layouts  8.66 us

profile of v1, /device:TPU:1, one launch (start us, length us, event | category | flops | bytes accessed | tf_op | source)
XLA Modules:
  0.0 64.9 jit_solution(341568799695826691)
XLA Ops:
  0.6 1.6 %copy.18.kg_hbm = bf16[512,64]{1,0:T(8,128)(2,1)} copy(bf16[512,64]{0,1:T(8,128)(2,1)} %param.15) | data formatting | bytes 131072 | tf_op args[1]
  2.2 1.6 %copy.19.vg_hbm = bf16[512,64]{1,0:T(8,128)(2,1)} copy(bf16[512,64]{0,1:T(8,128)(2,1)} %param.16) | data formatting | bytes 131072 | tf_op args[2]
  3.8 55.6 %bucket.1 = (f32[38,64]{1,0:T(8,128)}, f32[38,64]{1,0:T(8,128)}, f32[38,128]{1,0:T(8,128)}, bf16[1,4,64,128]{3,2,1,0:T(8,128)(2,1)}) custom-call(bf16[512,3584]{1,0:T(8,128)(2,1)} %hid_hbm.1, bf16[512,64]{1,0:T(8,128)(2,1)} %copy.18.kg_hbm, bf16[512,64]{1,0:T(8,128)(2,1)} %copy.19.vg_hbm, bf16[256,1024]{1,0:T(8,128)(2,1)} %vis_hbm.1, ...), custom_call_target="tpu_custom_call" | custom-call | tf_op jit(solution)/shard_map/bucket/pallas_call | solution.py:335
  59.4 1.3 %copy.24 = f32[38,64]{1,0:T(8,128)} copy(f32[38,64]{1,0:T(8,128)} %get-tuple-element.8) | data formatting | bytes 19456
  60.7 1.3 %copy.25 = f32[38,64]{1,0:T(8,128)} copy(f32[38,64]{1,0:T(8,128)} %get-tuple-element.9) | data formatting | bytes 19456
  62.1 1.3 %copy.26 = f32[38,128]{1,0:T(8,128)} copy(f32[38,128]{1,0:T(8,128)} %get-tuple-element.10) | data formatting | bytes 38912
  63.4 1.5 %copy.27 = bf16[1,4,64,128]{3,2,1,0:T(8,128)(2,1)} copy(bf16[1,4,64,128]{3,2,1,0:T(8,128)(2,1)} %get-tuple-element.11) | data formatting | bytes 131072

commit v2 on v1

v2 whole, which is shorter than its diff:
```python
import jax
import jax.numpy as jnp
from jax import lax
from jax.experimental import pallas as pl
from jax.experimental.pallas import tpu as pltpu
from jax.sharding import PartitionSpec as P

MESH = pl.DeviceIdType.MESH
F32 = jnp.float32
BF16 = jnp.bfloat16

NX, NY, NZ, NCORE, NHALF = 4, 8, 6, 2, 2
N_DP = NY * NZ * NCORE
N_CHIP = NY * NZ
SPREAD, CAP = 4, 64
SLOTS = SPREAD * CAP
IMAGES = 8
OWN = 38
BLK = 40
YROWS = NZ * NCORE * OWN
WIDE = 3584
FAR_Y = (4, 3, 5, 2, 6, 1, 7)
FAR_Z = ((5, 4, 3, 2, 1), (5, 4, 3, 0, 2), (5, 4, 0, 3, 1), (0, 1, 5, 2, 4), (0, 1, 2, 5, 3), (0, 1, 2, 3, 4))


def kernel(
    hid_hbm, kgt_hbm, vgt_hbm, vis_hbm, cot_hbm, gain_hbm, nb_hbm, w1_hbm, b1_hbm, w2_hbm, b2_hbm, ls_hbm,
    cnt_hbm, off_hbm,
    keyv, valv, projv, hand,
    hid, kvt, vis, cot, gain, nb, w1, b1, w2, b2, ls, cnt, off,
    packed, part, xs, xr, vs, vr, hs, hr, hpar,
    kvf, kvo, kvp, cotf, amat, apar, half,
    s1k, r1k, s2k, r2k, s1p, r1a, r1b, s2a, s2b, r2a, r2b,
    lsem, dsem_s, dsem_r, hpsem_s, hpsem_r, xsem_s, xsem_r, vsem_s, vsem_r, hsem_s, hsem_r,
    ky_s, ky_r, kz_s, kz_r, p1_s, p1_r, p2_s, p2_r, go,
):
    dp = lax.axis_index("dp")
    mp = lax.axis_index("mp")
    core = lax.rem(dp, NCORE)
    chip = lax.div(dp, NCORE)
    zlo = lax.rem(chip, NZ)
    y = lax.div(chip, NZ)
    zhi = lax.div(mp, NX)
    x = lax.rem(mp, NX)
    partner = (dp + 1 - 2 * core, mp)

    def rank_of(y_, z_):
        return (y_ * NZ + z_) * NCORE + core

    def far_z(i):
        to = jnp.int32(0)
        for q in range(NZ):
            to = jnp.where(zlo == q, FAR_Z[q][i], to)
        return to

    far = [far_z(i) for i in range(NZ - 1)]
    others = [lax.rem(zlo + d, NZ) for d in range(1, NZ)]

    def remote(src, dst, send, recv, who):
        return pltpu.make_async_remote_copy(
            src_ref=src, dst_ref=dst, send_sem=send, recv_sem=recv, device_id=who, device_id_type=MESH
        )

    loads = [
        (cnt_hbm, cnt), (off_hbm, off), (vis_hbm, vis), (gain_hbm, gain), (nb_hbm, nb), (w1_hbm, w1),
        (b1_hbm, b1), (w2_hbm, w2), (b2_hbm, b2), (ls_hbm, ls), (kgt_hbm, kvt.at[0:64]),
        (vgt_hbm, kvt.at[64:128]), (hid_hbm, hid), (cot_hbm.at[0], cot),
    ]
    copies = [pltpu.make_async_copy(s, d, lsem.at[i]) for i, (s, d) in enumerate(loads)]
    for c in copies[:12]:
        c.start()
    (l_cnt, l_off, l_vis, l_gain, l_nb, l_w1, l_b1, l_w2, l_b2, l_ls, l_kg, l_vg, l_hid, l_cot) = copies

    barrier = pltpu.get_barrier_semaphore()

    def greet(dp_, mp_):
        pl.semaphore_signal(barrier, 1, device_id=(dp_, mp_), device_id_type=MESH)

    for d in range(1, NX):
        greet(chip * NCORE, zhi * NX + lax.rem(x + d, NX))

    @pl.when(core == 1)
    def _():
        greet(chip * NCORE, mp)

    for d in range(1, NY):
        greet((lax.rem(y + d, NY) * NZ + zlo) * NCORE + 1, mp)
    for d in range(1, NZ):
        greet((y * NZ + lax.rem(zlo + d, NZ)) * NCORE + 1, mp)
    other = (1 - zhi) * NX + x
    for d in (0, 1, 2, N_CHIP - 1, N_CHIP - 2):
        there = lax.rem(chip + d, N_CHIP) * NCORE + 1
        if d:
            greet(there, mp)
        greet(there, other)
    near_count = 2 * (NX - 1) + 1
    far_count = 2 * (NY - 1 + NZ - 1 + 9)

    l_cnt.wait()
    l_off.wait()
    place = lax.broadcasted_iota(jnp.int32, (1, SLOTS), 1)
    target = jnp.full((1, SLOTS), -1, jnp.int32)
    counts = [cnt[0, i] for i in range(IMAGES)]
    offs = [off[0, i] for i in range(IMAGES)]
    start = jnp.int32(0)
    for i in range(IMAGES):
        end = start + counts[i]
        before = jnp.int32(0)
        for j in range(i):
            before = before + jnp.where(offs[j] == offs[i], counts[j], 0)
        base = (offs[i] - 1) * CAP + before - start
        inside = (place >= start) & (place < end)
        target = jnp.where(inside, place + base, target)
        start = end
    filled = []
    for k in range(1, SPREAD + 1):
        total = jnp.int32(0)
        for i in range(IMAGES):
            total = total + jnp.where(offs[i] == k, counts[i], 0)
        filled.append(total)
    slot_ids = lax.broadcasted_iota(jnp.int32, (SLOTS, SLOTS), 0)
    select = jnp.where(slot_ids == target, 1.0, 0.0).astype(BF16)

    l_vis.wait()
    packed[...] = jnp.dot(select, vis[...], preferred_element_type=F32).astype(BF16)
    values = packed[...].astype(F32)
    center = jnp.mean(values, axis=1, keepdims=True)
    delta = values - center
    spread_sq = jnp.mean(delta * delta, axis=1, keepdims=True)
    l_gain.wait()
    l_nb.wait()
    normed = (delta * lax.rsqrt(spread_sq + 1e-06) * gain[...] + nb[...]).astype(BF16)
    l_w1.wait()
    l_b1.wait()
    l_hid.start()
    pre = jnp.dot(normed, w1[...], preferred_element_type=F32) + b1[...]
    hidden = (0.5 * pre * (1.0 + lax.erf(pre * (0.5**0.5)))).astype(BF16)
    l_w2.wait()
    l_cot.start()

    def second(e):
        cols = pl.ds(pl.multiple_of(e * NX * 128, 128), NX * 128)
        res = jnp.dot(hidden, w2[:, cols], preferred_element_type=F32)
        part[e] = res
        for xd in range(NX):
            xs[e, xd] = res[:, xd * 128 : (xd + 1) * 128].astype(BF16).reshape(SPREAD, CAP, 128)

    second(1 - zhi)

    @pl.when(core == 0)
    def _():
        pl.semaphore_wait(barrier, near_count)
        pl.semaphore_signal(go.at[0], 1, device_id=partner, device_id_type=MESH)

    @pl.when(core == 1)
    def _():
        pl.semaphore_wait(go.at[0], 1)

    def x_copy(e, d, k):
        to = lax.rem(x + d, NX)
        return remote(
            xs.at[e, to, k], xr.at[e, d - 1, k], xsem_s.at[e, d - 1, k], xsem_r.at[e, d - 1, k],
            (dp, zhi * NX + to),
        )

    for k in range(SPREAD):
        for d in (2, 1, 3):
            x_copy(1 - zhi, d, k).start()
    second(zhi)
    for k in range(SPREAD):
        for d in (2, 1, 3):
            x_copy(zhi, d, k).start()

    own_cols = pl.ds(pl.multiple_of(mp * 128, 128), 128)
    for k in range(SPREAD):
        vs[k] = packed[k * CAP : (k + 1) * CAP, own_cols]

    l_kg.wait()
    l_vg.wait()
    l_hid.wait()
    kv = kvt[...].astype(F32).T.astype(BF16)

    @pl.loop(0, 7)
    def _(i):
        cols = pl.ds(pl.multiple_of(i * 512, 512), 512)
        kvf[cols, :] = lax.dot_general(
            hid[:, cols], kv, (((0,), (0,)), ((), ())), preferred_element_type=F32
        )

    colsum = jnp.sum(kv.astype(F32), axis=0, keepdims=True)
    tail_row = lax.broadcasted_iota(jnp.int32, (80, 128), 0)
    kvf[WIDE : WIDE + 80, :] = jnp.where(tail_row == 0, colsum, 0.0)

    @pl.loop(0, NY)
    def _(yy):
        win = kvf[pl.ds(pl.multiple_of(yy * YROWS, 8), YROWS + 8), :]
        for z in range(NZ):
            for c in range(NCORE):
                at = (z * NCORE + c) * OWN
                kvo[c, yy, z] = win[at : at + BLK, :]

    kv_swap = remote(kvo.at[1 - core], kvp, dsem_s.at[0], dsem_r.at[0], partner)
    kv_swap.start()

    def v_copy(k):
        return remote(vs.at[k], vr.at[k], vsem_s.at[k], vsem_r.at[k], (lax.rem(dp + k + 1, N_DP), mp))

    def h_copy(e, k):
        to = (lax.rem(dp + k + 1, N_DP), e * NX + x)
        return remote(hs.at[e, k], hr.at[zhi, k], hsem_s.at[e, k], hsem_r.at[zhi, k], to)

    def h_wait(e, k):
        to = (lax.rem(dp + k + 1, N_DP), e * NX + x)
        remote(hs.at[e, k], hr.at[e, k], hsem_s.at[e, k], hsem_r.at[e, k], to).wait_recv()

    l_b2.wait()
    l_ls.wait()
    with_bias = jnp.where(zhi == 0, 1.0, 0.0)
    slot_in = lax.broadcasted_iota(jnp.int32, (CAP, 128), 0)
    @pl.when(core == 1)
    def _():
        pl.semaphore_wait(barrier, far_count)
        pl.semaphore_signal(go.at[1], 1, device_id=partner, device_id_type=MESH)

    @pl.when(core == 0)
    def _():
        pl.semaphore_wait(go.at[1], 1)

    for k in range(SPREAD):
        v_copy(k).start()

    def sum_x(e):
        cols = pl.ds(pl.multiple_of((e * NX + x) * 128, 128), 128)
        own = pl.ds(pl.multiple_of(x * 128, 128), 128)
        for k in range(SPREAD):
            for d in range(1, NX):
                x_copy(e, d, k).wait_recv()
            total = part[e, k * CAP : (k + 1) * CAP, own]
            for d in range(1, NX):
                total = total + xr[e, d - 1, k].astype(F32)
            branch = ls[:, cols] * (total + with_bias * b2[:, cols])
            hs[e, k] = jnp.where(slot_in < filled[k], branch, 0.0).astype(BF16)
            h_copy(e, k).start()

    sum_x(1 - zhi)
    sum_x(zhi)

    def ky_copy(d):
        to = lax.rem(y + d, NY)
        return remote(s1k.at[to], r1k.at[d - 1], ky_s.at[d - 1], ky_r.at[d - 1], (rank_of(to, zlo), mp))

    def kz_copy(to):
        return remote(s2k.at[to], r2k.at[zlo], kz_s.at[to], kz_r.at[zlo], (rank_of(y, to), mp))

    def kz_wait(q):
        remote(s2k.at[q], r2k.at[q], kz_s.at[q], kz_r.at[q], (rank_of(y, q), mp)).wait_recv()

    kv_swap.wait()

    @pl.loop(0, NY)
    def _(yy):
        s1k[yy] = (kvo[core, yy] + kvp[yy]).astype(BF16)

    for d in FAR_Y:
        ky_copy(d).start()

    l_cot.wait()

    @pl.loop(0, 28)
    def _(i):
        cols = pl.ds(pl.multiple_of(i * 128, 128), 128)
        block = cot[:, :, cols].reshape(SLOTS, 128).astype(F32)
        cotf[cols, :] = block.T

    cotf[WIDE : WIDE + 80, :] = jnp.zeros((80, SLOTS), F32)

    @pl.loop(0, NY // 2)
    def _(j):
        win = cotf[pl.ds(pl.multiple_of(j * 2 * YROWS, 8), 2 * YROWS + 8), :]

        def block(yy, z, c):
            at = yy * YROWS + (z * NCORE + c) * OWN
            return win[at : at + BLK, :]

        for yy in range(2):
            rows = jnp.concatenate([block(yy, z, 0) for z in range(NZ)], axis=0).astype(BF16)
            amat[0, pl.ds(pl.multiple_of((2 * j + yy) * NZ * BLK, 16), NZ * BLK), :] = rows
        for z in range(NZ):
            rows = jnp.concatenate([block(0, z, 1), block(1, z, 1)], axis=0).astype(BF16)
            amat[1, pl.ds(pl.multiple_of((z * NY + 2 * j) * BLK, 16), 2 * BLK), :] = rows

    a_swap = remote(amat.at[1 - core], apar, dsem_s.at[1], dsem_r.at[1], partner)
    a_swap.start()

    def hp_copy(k):
        return remote(hand.at[0, k], hpar.at[k], hpsem_s.at[k], hpsem_r.at[k], partner)

    for k in range(SPREAD):
        v_copy(k).wait_recv()
        for e in range(NHALF):
            h_wait(e, k)
        hand[0, k] = (vr[k].astype(F32) + (hr[0, k].astype(F32) + hr[1, k].astype(F32))).astype(BF16)
        hp_copy(k).start()

    half[...] = jnp.dot(amat[core], hand[0].reshape(SLOTS, 128), preferred_element_type=F32)

    a_swap.wait_recv()
    for k in range(SPREAD):
        hp_copy(k).wait_recv()

    theirs = hpar[...].reshape(SLOTS, 128)

    def p1y_copy(d):
        to = lax.rem(y + d, NY)
        return remote(
            s1p.at[pl.ds(to * NZ, NZ)], r1a.at[d - 1], p1_s.at[d - 1], p1_r.at[d - 1], (rank_of(to, zlo), mp)
        )

    def p1z_copy(to):
        return remote(s1p.at[pl.ds(to * NY, NY)], r1b.at[zlo], p1_s.at[to], p1_r.at[zlo], (rank_of(y, to), mp))

    def p1z_wait(q):
        remote(s1p.at[pl.ds(q * NY, NY)], r1b.at[q], p1_s.at[q], p1_r.at[q], (rank_of(y, q), mp)).wait_recv()

    def p2z_copy(to):
        return remote(s2a.at[to], r2a.at[zlo], p2_s.at[to], p2_r.at[zlo], (rank_of(y, to), mp))

    def p2z_wait(q):
        remote(s2a.at[q], r2a.at[q], p2_s.at[q], p2_r.at[q], (rank_of(y, q), mp)).wait_recv()

    def p2y_copy(d):
        to = lax.rem(y + d, NY)
        return remote(s2b.at[to], r2b.at[d - 1], p2_s.at[d - 1], p2_r.at[d - 1], (rank_of(to, zlo), mp))

    def block_rows(to, count):
        rows = pl.ds(pl.multiple_of(to * count * BLK, 16), count * BLK)
        res = half[rows, :] + jnp.dot(apar[rows, :], theirs, preferred_element_type=F32)
        for i in range(count):
            s1p[to * count + i] = res[i * BLK : (i + 1) * BLK, :].astype(BF16)

    @pl.when(core == 0)
    def _():
        for d in FAR_Y:
            block_rows(lax.rem(y + d, NY), NZ)
            p1y_copy(d).start()
        block_rows(y, NZ)

    @pl.when(core == 1)
    def _():
        for to in far:
            block_rows(to, NY)
            p1z_copy(to).start()
        block_rows(zlo, NY)

    total = s1k[y].astype(F32)
    for d in FAR_Y[::-1]:
        ky_copy(d).wait_recv()
        total = total + r1k[d - 1].astype(F32)
    s2k[...] = total.astype(BF16)
    for to in far:
        kz_copy(to).start()

    @pl.when(core == 0)
    def _():
        total = s1p[pl.ds(y * NZ, NZ)].astype(F32)
        for d in FAR_Y[::-1]:
            p1y_copy(d).wait_recv()
            total = total + r1a[d - 1].astype(F32)
        s2a[...] = total.astype(BF16)
        for to in far:
            p2z_copy(to).start()

    @pl.when(core == 1)
    def _():
        total = s1p[pl.ds(zlo * NY, NY)].astype(F32)
        for q in others:
            p1z_wait(q)
            total = total + r1b[q].astype(F32)
        s2b[...] = total.astype(BF16)
        for d in FAR_Y:
            p2y_copy(d).start()

    total = s2k[zlo].astype(F32)
    for q in others:
        kz_wait(q)
        total = total + r2k[q].astype(F32)
    keyv[...] = total[:OWN, :64]
    valv[...] = total[:OWN, 64:]

    a_swap.wait_send()
    for k in range(SPREAD):
        for d in range(1, NX):
            for e in range(NHALF):
                x_copy(e, d, k).wait_send()
        v_copy(k).wait_send()
        hp_copy(k).wait_send()
        for e in range(NHALF):
            h_copy(e, k).wait_send()
    for d in range(1, NY):
        ky_copy(d).wait_send()
    for q in others:
        kz_copy(q).wait_send()

    @pl.when(core == 0)
    def _():
        for d in range(1, NY):
            p1y_copy(d).wait_send()
        for q in others:
            p2z_copy(q).wait_send()

    @pl.when(core == 1)
    def _():
        for q in others:
            p1z_copy(q).wait_send()
        for d in range(1, NY):
            p2y_copy(d).wait_send()

    @pl.when(core == 0)
    def _():
        total = s2a[zlo].astype(F32)
        for q in others:
            p2z_wait(q)
            total = total + r2a[q].astype(F32)
        projv[...] = total[:OWN, :]

    @pl.when(core == 1)
    def _():
        total = s2b[y].astype(F32)
        for d in FAR_Y[::-1]:
            p2y_copy(d).wait_recv()
            total = total + r2b[d - 1].astype(F32)
        projv[...] = total[:OWN, :]


def writer(key_i, val_i, proj_i, hand_i, key_o, val_o, proj_o, hand_o, sem):
    pairs = ((key_i, key_o), (val_i, val_o), (proj_i, proj_o), (hand_i, hand_o))
    copies = [pltpu.make_async_copy(s, d, sem.at[i]) for i, (s, d) in enumerate(pairs)]
    for c in copies:
        c.start()
    for c in copies:
        c.wait()


def per_device(
    hidden_rows, key_grad, value_grad, visual_rows, visual_cotangent, norm_gain, norm_bias,
    fc1_weight, fc1_bias, fc2_weight, fc2_bias, layer_scale, token_counts, dest_offsets,
):
    anyspec = pl.BlockSpec(memory_space=pl.ANY)
    vmem = pl.BlockSpec(memory_space=pltpu.VMEM)
    dma = pltpu.SemaphoreType.DMA
    V = pltpu.VMEM
    S = pltpu.SMEM
    scratch = [
        V((512, WIDE), BF16), V((128, 512), BF16), V((256, 1024), BF16), V((4, 64, WIDE), BF16),
        V((1, 1024), F32), V((1, 1024), F32), V((1024, 512), BF16), V((1, 512), F32),
        V((512, 1024), BF16), V((1, 1024), F32), V((1, 1024), F32),
        S((1, IMAGES), jnp.int32), S((1, IMAGES), jnp.int32),
        V((256, 1024), BF16), V((NHALF, 256, 512), F32),
        V((NHALF, NX, SPREAD, CAP, 128), BF16), V((NHALF, NX - 1, SPREAD, CAP, 128), BF16),
        V((SPREAD, CAP, 128), BF16), V((SPREAD, CAP, 128), BF16),
        V((NHALF, SPREAD, CAP, 128), BF16), V((NHALF, SPREAD, CAP, 128), BF16),
        V((SPREAD, CAP, 128), BF16),
        V((WIDE + 80, 128), F32), V((NCORE, NY, NZ, BLK, 128), F32), V((NY, NZ, BLK, 128), F32),
        V((WIDE + 80, 256), F32), V((NCORE, N_CHIP * BLK, 256), BF16), V((N_CHIP * BLK, 256), BF16),
        V((N_CHIP * BLK, 128), F32),
        V((NY, NZ, BLK, 128), BF16), V((NY - 1, NZ, BLK, 128), BF16),
        V((NZ, BLK, 128), BF16), V((NZ, BLK, 128), BF16),
        V((N_CHIP, BLK, 128), BF16), V((NY - 1, NZ, BLK, 128), BF16), V((NZ, NY, BLK, 128), BF16),
        V((NZ, BLK, 128), BF16), V((NY, BLK, 128), BF16), V((NZ, BLK, 128), BF16), V((NY - 1, BLK, 128), BF16),
        dma((14,)), dma((2,)), dma((2,)), dma((SPREAD,)), dma((SPREAD,)),
        dma((NHALF, NX - 1, SPREAD)), dma((NHALF, NX - 1, SPREAD)), dma((SPREAD,)), dma((SPREAD,)),
        dma((NHALF, SPREAD)), dma((NHALF, SPREAD)),
        dma((NY - 1,)), dma((NY - 1,)), dma((NZ,)), dma((NZ,)),
        dma((NY - 1,)), dma((NY - 1,)), dma((NY - 1,)), dma((NY - 1,)), pltpu.SemaphoreType.REGULAR((2,)),
    ]
    shapes = (
        jax.ShapeDtypeStruct((OWN, 64), F32),
        jax.ShapeDtypeStruct((OWN, 64), F32),
        jax.ShapeDtypeStruct((OWN, 128), F32),
        jax.ShapeDtypeStruct((1, SPREAD, CAP, 128), BF16),
    )
    results = pl.pallas_call(
        kernel,
        out_shape=shapes,
        in_specs=[anyspec] * 14,
        out_specs=[vmem] * 4,
        scratch_shapes=scratch,
        compiler_params=pltpu.CompilerParams(
            collective_id=0, has_side_effects=True, vmem_limit_bytes=60 * 1024 * 1024
        ),
        name="bucket",
    )(
        hidden_rows, key_grad.T, value_grad.T, visual_rows, visual_cotangent,
        norm_gain.reshape(1, -1), norm_bias.reshape(1, -1), fc1_weight, fc1_bias.reshape(1, -1),
        fc2_weight, fc2_bias.reshape(1, -1), layer_scale.reshape(1, -1), token_counts, dest_offsets,
    )
    return pl.pallas_call(
        writer,
        out_shape=shapes,
        in_specs=[vmem] * 4,
        out_specs=[anyspec] * 4,
        scratch_shapes=[dma((4,))],
        name="writer",
    )(*results)


def solution(mesh):
    placed = (
        P("dp", None), P("dp", "mp"), P("dp", "mp"), P("dp", None), P("dp", None, None, None),
        P(), P(), P(None, "mp"), P("mp"), P("mp", None), P(), P(), P("dp", None), P("dp", None),
    )
    return jax.shard_map(
        per_device,
        mesh=mesh,
        in_specs=placed,
        out_specs=(P("dp", "mp"), P("dp", "mp"), P("dp", "mp"), P("dp", None, None, "mp")),
        check_vma=False,
    )
```

time: 65.3 us -> 50.1 us (0.77)
  the two profiles are of different devices: /device:TPU:1 before, /device:TPU:65 now
where the time goes in v2:
time: 50.1 us; the launch traced here: 49.9 us
  Pallas kernels  49.3 us (98%)
  between operations  0.64 us (1%)
    pallas_call x1, Pallas kernels, per_device(): pl.pallas_call(kernel, out_shape=shapes, in_specs=[anyspec] * 14, out_spe...  47.7 us
    pallas_call x1, Pallas kernels, per_device(): pl.pallas_call(writer, out_shape=shapes, in_specs=[vmem] * 4, out_specs=[...  1.58 us

profile of v2, /device:TPU:65, one launch (start us, length us, event | category | flops | bytes accessed | tf_op | source)
XLA Modules:
  0.0 49.9 jit_solution(14636472190926404660)
XLA Ops:
  0.6 47.7 %bucket.1 = (f32[38,64]{1,0:T(8,128)}, f32[38,64]{1,0:T(8,128)}, f32[38,128]{1,0:T(8,128)}, bf16[1,4,64,128]{3,2,1,0:T(8,128)(2,1)}) custom-call(bf16[512,3584]{1,0:T(8,128)(2,1)} %hid_hbm.1, bf16[64,512]{1,0:T(8,128)(2,1)} %bitcast.7, bf16[64,512]{1,0:T(8,128)(2,1)} %bitcast.8, bf16[256,1024]{1,0:T(8,128)(2,1)} %vis_hbm.1, ...), custom_call_target="tpu_custom_call" | custom-call | tf_op jit(solution)/shard_map/bucket/pallas_call | solution.py:482
  48.4 1.6 %writer.1 = (f32[38,64]{1,0:T(8,128)}, f32[38,64]{1,0:T(8,128)}, f32[38,128]{1,0:T(8,128)}, bf16[1,4,64,128]{3,2,1,0:T(8,128)(2,1)}) custom-call(f32[38,64]{1,0:T(8,128)} %get-tuple-element.8.key_i, f32[38,64]{1,0:T(8,128)} %get-tuple-element.9.val_i, f32[38,128]{1,0:T(8,128)} %get-tuple-element.10.proj_i, bf16[1,4,64,128]{3,2,1,0:T(8,128)(2,1)} %get-tuple-element.11.hand_i), custom_call_target="tpu_custom_call" | custom-call | tf_op jit(solution)/shard_map/writer/pallas_call | solution.py:497

commit v3 on v2

v3 whole, which is shorter than its diff:
```python
import jax
import jax.numpy as jnp
from jax import lax
from jax.experimental import pallas as pl
from jax.experimental.pallas import tpu as pltpu
from jax.sharding import PartitionSpec as P

MESH = pl.DeviceIdType.MESH
F32 = jnp.float32
BF16 = jnp.bfloat16

NX, NY, NZ, NCORE, NHALF = 4, 8, 6, 2, 2
N_DP = NY * NZ * NCORE
N_CHIP = NY * NZ
SPREAD, CAP = 4, 64
SLOTS = SPREAD * CAP
IMAGES = 8
OWN = 38
BLK = 40
YROWS = NZ * NCORE * OWN
WIDE = 3584
FAR_Y = (4, 3, 5, 2, 6, 1, 7)
CHUNK = 4
GROUPS = ((0, 1), (1, 2), (3, 3))
EDGES = (0, NZ - 1)
FAR_Z = ((5, 4, 3, 2, 1), (5, 4, 3, 0, 2), (5, 4, 0, 3, 1), (0, 1, 5, 2, 4), (0, 1, 2, 5, 3), (0, 1, 2, 3, 4))


def kernel(
    hid_hbm, kgt_hbm, vgt_hbm, vis_hbm, cot_hbm, gain_hbm, nb_hbm, w1_hbm, b1_hbm, w2_hbm, b2_hbm, ls_hbm,
    cnt_hbm, off_hbm,
    keyv, valv, projv, hand,
    hid, kvt, vis, cot, vecs, w1, b1, w2, table,
    packed, hidden, part, xs, xr, vs, hs, got, hpar,
    kvf, kvo, kvp, cotf, amat, apar, half,
    s1k, r1k, s2k, r2k, s1p, r1y, r1z, s2z, s2y, r2z, r2y,
    lsem, swap_s, swap_r, x_s, x_r, got_s, got_r, k_s, k_r, p1y_s, p1y_r, p_s, p_r, go,
):
    dp = lax.axis_index("dp")
    mp = lax.axis_index("mp")
    core = lax.rem(dp, NCORE)
    chip = lax.div(dp, NCORE)
    zlo = lax.rem(chip, NZ)
    y = lax.div(chip, NZ)
    zhi = lax.div(mp, NX)
    x = lax.rem(mp, NX)
    partner = (dp + 1 - 2 * core, mp)

    def rank_of(y_, z_):
        return (y_ * NZ + z_) * NCORE + core

    def far_z(i):
        to = jnp.int32(0)
        for q in range(NZ):
            to = jnp.where(zlo == q, FAR_Z[q][i], to)
        return to

    far = [far_z(i) for i in range(NZ - 1)]

    def remote(src, dst, send, recv, who):
        return pltpu.make_async_remote_copy(
            src_ref=src, dst_ref=dst, send_sem=send, recv_sem=recv, device_id=who, device_id_type=MESH
        )

    def arrived(ref, sem):
        pltpu.make_async_copy(ref, ref, sem).wait()

    def load(i, *pairs):
        for src, dst in pairs:
            pltpu.make_async_copy(src, dst, lsem.at[i]).start()

    load(0, (cnt_hbm, table.at[0:1]), (off_hbm, table.at[1:2]))
    load(1, (vis_hbm, vis))
    load(2, *[(v, vecs.at[i : i + 1]) for i, v in enumerate((gain_hbm, nb_hbm, b2_hbm, ls_hbm))])
    load(3, (w1_hbm, w1))
    load(4, (b1_hbm, b1))
    load(5, (w2_hbm, w2))
    load(6, (kgt_hbm, kvt.at[0:64]), (vgt_hbm, kvt.at[64:128]))

    barrier = pltpu.get_barrier_semaphore()

    def greet(dp_, mp_):
        pl.semaphore_signal(barrier, 1, device_id=(dp_, mp_), device_id_type=MESH)

    for d in range(1, NX):
        greet(chip * NCORE, zhi * NX + lax.rem(x + d, NX))

    @pl.when(core == 1)
    def _():
        greet(chip * NCORE, mp)

    for d in range(1, NY):
        greet((lax.rem(y + d, NY) * NZ + zlo) * NCORE + 1, mp)
    for d in range(1, NZ):
        greet((y * NZ + lax.rem(zlo + d, NZ)) * NCORE + 1, mp)
    other = (1 - zhi) * NX + x
    for d in (0, 1, 2, N_CHIP - 1, N_CHIP - 2):
        there = lax.rem(chip + d, N_CHIP) * NCORE + 1
        if d:
            greet(there, mp)
        greet(there, other)
    near_count = 2 * (NX - 1) + 1
    far_count = 2 * (NY - 1 + NZ - 1 + 9)

    arrived(table, lsem.at[0])
    place = lax.broadcasted_iota(jnp.int32, (1, SLOTS), 1)
    target = jnp.full((1, SLOTS), -1, jnp.int32)
    counts = [table[0, i] for i in range(IMAGES)]
    offs = [table[1, i] for i in range(IMAGES)]
    start = jnp.int32(0)
    for i in range(IMAGES):
        end = start + counts[i]
        before = jnp.int32(0)
        for j in range(i):
            before = before + jnp.where(offs[j] == offs[i], counts[j], 0)
        base = (offs[i] - 1) * CAP + before - start
        inside = (place >= start) & (place < end)
        target = jnp.where(inside, place + base, target)
        start = end
    filled = []
    for k in range(1, SPREAD + 1):
        total = jnp.int32(0)
        for i in range(IMAGES):
            total = total + jnp.where(offs[i] == k, counts[i], 0)
        filled.append(total)
    slot_ids = lax.broadcasted_iota(jnp.int32, (SLOTS, SLOTS), 0)
    select = jnp.where(slot_ids == target, 1.0, 0.0).astype(BF16)

    def x_copy(e, d, k):
        to = lax.rem(x + d, NX)
        return remote(
            xs.at[e, to, k], xr.at[e, k, d - 1], x_s.at[0], x_r.at[e, k], (dp, zhi * NX + to)
        )

    def second(e, first, count):
        rows = slice(first * CAP, (first + count) * CAP)
        cols = pl.ds(pl.multiple_of(e * NX * 128, 128), NX * 128)
        res = jnp.dot(hidden[rows], w2[:, cols], preferred_element_type=F32)
        part[e, rows] = res
        for xd in range(NX):
            xs[e, xd, first : first + count] = (
                res[:, xd * 128 : (xd + 1) * 128].astype(BF16).reshape(count, CAP, 128)
            )

    def send_x(e, first, count):
        for k in range(first, first + count):
            for d in (2, 1, 3):
                x_copy(e, d, k).start()

    arrived(vis, lsem.at[1])
    for first in range(0, SPREAD, CHUNK):
        rows = slice(first * CAP, (first + CHUNK) * CAP)
        placed = jnp.dot(select[rows], vis[...], preferred_element_type=F32)
        packed[rows] = placed.astype(BF16)
        center = jnp.mean(placed, axis=1, keepdims=True)
        delta = placed - center
        spread_sq = jnp.mean(delta * delta, axis=1, keepdims=True)
        if first == 0:
            arrived(vecs, lsem.at[2])
        normed = (delta * lax.rsqrt(spread_sq + 1e-06) * vecs[0:1, :] + vecs[1:2, :]).astype(BF16)
        if first == 0:
            arrived(w1, lsem.at[3])
            arrived(b1, lsem.at[4])
            load(7, (hid_hbm, hid))
        pre = jnp.dot(normed, w1[...], preferred_element_type=F32) + b1[...]
        hidden[rows] = (0.5 * pre * (1.0 + lax.erf(pre * (0.5**0.5)))).astype(BF16)
        if first == 0:
            arrived(w2, lsem.at[5])
            load(8, (cot_hbm.at[0], cot))
        second(0, first, CHUNK)
        if first == 0:
            @pl.when(core == 0)
            def _():
                pl.semaphore_wait(barrier, near_count)
                pl.semaphore_signal(go.at[0], 1, device_id=partner, device_id_type=MESH)

            @pl.when(core == 1)
            def _():
                pl.semaphore_wait(go.at[0], 1)
        send_x(0, first, CHUNK)
    second(1, 0, SPREAD)
    send_x(1, 0, SPREAD)

    own_cols = pl.ds(pl.multiple_of(mp * 128, 128), 128)
    for k in range(SPREAD):
        vs[k] = packed[k * CAP : (k + 1) * CAP, own_cols]

    arrived(kvt, lsem.at[6])
    arrived(hid, lsem.at[7])
    kv = kvt[...].astype(F32).T.astype(BF16)

    @pl.loop(0, 7)
    def _(i):
        cols = pl.ds(pl.multiple_of(i * 512, 512), 512)
        kvf[cols, :] = lax.dot_general(
            hid[:, cols], kv, (((0,), (0,)), ((), ())), preferred_element_type=F32
        )

    colsum = jnp.sum(kv.astype(F32), axis=0, keepdims=True)
    tail_row = lax.broadcasted_iota(jnp.int32, (80, 128), 0)
    kvf[WIDE : WIDE + 80, :] = jnp.where(tail_row == 0, colsum, 0.0)

    @pl.loop(0, NY)
    def _(yy):
        win = kvf[pl.ds(pl.multiple_of(yy * YROWS, 8), YROWS + 8), :]
        for z in range(NZ):
            for c in range(NCORE):
                at = (z * NCORE + c) * OWN
                kvo[c, yy, z] = win[at : at + BLK, :]

    kv_swap = remote(kvo.at[1 - core], kvp, swap_s.at[0], swap_r.at[0], partner)
    kv_swap.start()

    def v_copy(k):
        return remote(vs.at[k], got.at[k, 2], got_s.at[0], got_r.at[k], (lax.rem(dp + k + 1, N_DP), mp))

    def h_copy(e, k):
        to = (lax.rem(dp + k + 1, N_DP), e * NX + x)
        return remote(hs.at[e, k], got.at[k, zhi], got_s.at[0], got_r.at[k], to)

    with_bias = jnp.where(zhi == 0, 1.0, 0.0)
    slot_in = lax.broadcasted_iota(jnp.int32, (CAP, 128), 0)
    @pl.when(core == 1)
    def _():
        pl.semaphore_wait(barrier, far_count)
        pl.semaphore_signal(go.at[1], 1, device_id=partner, device_id_type=MESH)

    @pl.when(core == 0)
    def _():
        pl.semaphore_wait(go.at[1], 1)

    def sum_x(e):
        cols = pl.ds(pl.multiple_of((e * NX + x) * 128, 128), 128)
        own = pl.ds(pl.multiple_of(x * 128, 128), 128)
        for k in range(SPREAD):
            arrived(xr.at[e, k], x_r.at[e, k])
            total = part[e, k * CAP : (k + 1) * CAP, own]
            for d in range(1, NX):
                total = total + xr[e, k, d - 1].astype(F32)
            branch = vecs[3:4, cols] * (total + with_bias * vecs[2:3, cols])
            hs[e, k] = jnp.where(slot_in < filled[k], branch, 0.0).astype(BF16)
            h_copy(e, k).start()

    def send_v():
        for k in range(SPREAD):
            v_copy(k).start()

    sum_x(0)
    pl.when(zhi == 0)(send_v)
    def ky_copy(d):
        to = lax.rem(y + d, NY)
        return remote(s1k.at[to], r1k.at[d - 1], k_s.at[0], k_r.at[0], (rank_of(to, zlo), mp))

    def from_z(to):
        return lax.rem(zlo - to + NZ, NZ) - 1

    def kz_copy(to):
        return remote(s2k.at[to], r2k.at[from_z(to)], k_s.at[1], k_r.at[1], (rank_of(y, to), mp))

    kv_swap.wait()

    @pl.loop(0, NY)
    def _(yy):
        s1k[yy] = (kvo[core, yy] + kvp[yy]).astype(BF16)

    for d in FAR_Y:
        ky_copy(d).start()

    sum_x(1)
    pl.when(zhi == 1)(send_v)

    arrived(cot, lsem.at[8])

    @pl.loop(0, 28)
    def _(i):
        cols = pl.ds(pl.multiple_of(i * 128, 128), 128)
        block = cot[:, :, cols].reshape(SLOTS, 128).astype(F32)
        cotf[cols, :] = block.T

    cotf[WIDE : WIDE + 80, :] = jnp.zeros((80, SLOTS), F32)

    @pl.loop(0, NY // 2)
    def _(j):
        win = cotf[pl.ds(pl.multiple_of(j * 2 * YROWS, 8), 2 * YROWS + 8), :]

        def block(yy, z, c):
            at = yy * YROWS + (z * NCORE + c) * OWN
            return win[at : at + BLK, :]

        for c in range(NCORE):
            for z in range(NZ):
                rows = jnp.concatenate([block(0, z, c), block(1, z, c)], axis=0).astype(BF16)
                amat[c, pl.ds(pl.multiple_of((z * NY + 2 * j) * BLK, 16), 2 * BLK), :] = rows

    a_swap = remote(amat.at[1 - core], apar, swap_s.at[1], swap_r.at[1], partner)
    a_swap.start()

    def hp_copy(k):
        return remote(hand.at[0, k], hpar.at[k], swap_s.at[2], swap_r.at[2], partner)

    for k in range(SPREAD):
        arrived(got.at[k], got_r.at[k])
        branch = got[k, 0].astype(F32) + got[k, 1].astype(F32)
        hand[0, k] = (got[k, 2].astype(F32) + branch).astype(BF16)
        hp_copy(k).start()

    half[...] = jnp.dot(amat[core], hand[0].reshape(SLOTS, 128), preferred_element_type=F32)

    a_swap.wait_recv()
    arrived(hpar, swap_r.at[2])

    theirs = hpar[...].reshape(SLOTS, 128)

    def p1y_copy(d, i, first, count):
        to = lax.rem(y + d, NY)
        zs = pl.ds(first, count)
        return remote(
            s1p.at[zs, to], r1y.at[d - 1, zs], p1y_s.at[i], p1y_r.at[i], (rank_of(to, zlo), mp)
        )

    def p1z_copy(to):
        return remote(s1p.at[to], r1z.at[from_z(to)], p_s.at[0], p_r.at[0], (rank_of(y, to), mp))

    def p2z_copy(to):
        return remote(s2z.at[to], r2z.at[from_z(to)], p_s.at[1], p_r.at[1], (rank_of(y, to), mp))

    def p2y_copy(d):
        to = lax.rem(y + d, NY)
        return remote(s2y.at[to], r2y.at[d - 1], p_s.at[2], p_r.at[2], (rank_of(to, zlo), mp))

    def block_rows(z):
        rows = pl.ds(pl.multiple_of(z * NY * BLK, 16), NY * BLK)
        res = half[rows, :] + jnp.dot(apar[rows, :], theirs, preferred_element_type=F32)
        s1p[z] = res.astype(BF16).reshape(NY, BLK, 128)

    inner = (zlo > 0) & (zlo < NZ - 1)
    z_first = (core == 1) & inner

    @pl.when(core == 0)
    def _():
        for i, (first, count) in enumerate(GROUPS):
            for z in range(first, first + count):
                block_rows(z)
            for d in FAR_Y:
                p1y_copy(d, i, first, count).start()

    @pl.when(core == 1)
    def _():
        for i, z in enumerate(EDGES):
            block_rows(z)
            for d in FAR_Y:
                p1y_copy(d, i, z, 1).start()
            if i == 0:
                for to in far:
                    @pl.when((to > 0) & (to < NZ - 1))
                    def _():
                        block_rows(to)
                        p1z_copy(to).start()

                @pl.when(inner)
                def _():
                    block_rows(zlo)

    total = s1k[y].astype(F32)
    arrived(r1k, k_r.at[0])
    for d in range(1, NY):
        total = total + r1k[d - 1].astype(F32)
    s2k[...] = total.astype(BF16)
    for to in far:
        kz_copy(to).start()

    def sum_y(i, first, count):
        total = s1p[first : first + count, y].astype(F32)
        arrived(r1y.at[:, pl.ds(first, count)], p1y_r.at[i])
        for d in range(1, NY):
            total = total + r1y[d - 1, first : first + count].astype(F32)
        s2z[first : first + count] = total.astype(BF16)
        for z in range(first, first + count):
            @pl.when(zlo != z)
            def _():
                p2z_copy(z).start()

    @pl.when(core == 0)
    def _():
        for i, (first, count) in enumerate(GROUPS):
            sum_y(i, first, count)

    @pl.when(core == 1)
    def _():
        sum_y(0, EDGES[0], 1)

        @pl.when(inner)
        def _():
            total = s1p[zlo].astype(F32)
            arrived(r1z, p_r.at[0])
            for d in range(1, NZ):
                total = total + r1z[d - 1].astype(F32)
            s2y[...] = total.astype(BF16)
            for d in FAR_Y:
                p2y_copy(d).start()

        sum_y(1, EDGES[1], 1)

    total = s2k[zlo].astype(F32)
    arrived(r2k, k_r.at[1])
    for d in range(1, NZ):
        total = total + r2k[d - 1].astype(F32)
    keyv[...] = total[:OWN, :64]
    valv[...] = total[:OWN, 64:]

    a_swap.wait_send()
    arrived(hpar, swap_s.at[2])
    arrived(xr, x_s.at[0])
    arrived(got, got_s.at[0])
    arrived(r1k, k_s.at[0])
    arrived(r2k, k_s.at[1])

    @pl.when(core == 0)
    def _():
        for i, (first, count) in enumerate(GROUPS):
            arrived(r1y.at[:, pl.ds(first, count)], p1y_s.at[i])
        arrived(r2z, p_s.at[1])

    @pl.when(core == 1)
    def _():
        for i, z in enumerate(EDGES):
            arrived(r1y.at[:, pl.ds(z, 1)], p1y_s.at[i])

        @pl.when(inner)
        def _():
            arrived(r1z.at[0 : NZ - 3], p_s.at[0])
            arrived(s2z.at[0:2], p_s.at[1])

        @pl.when(jnp.logical_not(inner))
        def _():
            arrived(r1z.at[0 : NZ - 2], p_s.at[0])
            arrived(s2z.at[0:1], p_s.at[1])

    @pl.when(z_first)
    def _():
        total = s2y[y].astype(F32)
        arrived(r2y, p_r.at[2])
        for d in range(1, NY):
            total = total + r2y[d - 1].astype(F32)
        projv[...] = total[:OWN, :]
        arrived(r2y, p_s.at[2])

    @pl.when(jnp.logical_not(z_first))
    def _():
        total = s2z[zlo].astype(F32)
        arrived(r2z, p_r.at[1])
        for d in range(1, NZ):
            total = total + r2z[d - 1].astype(F32)
        projv[...] = total[:OWN, :]


def writer(key_i, val_i, proj_i, hand_i, key_o, val_o, proj_o, hand_o, sem):
    pairs = ((key_i, key_o), (val_i, val_o), (proj_i, proj_o), (hand_i, hand_o))
    copies = [pltpu.make_async_copy(s, d, sem.at[i]) for i, (s, d) in enumerate(pairs)]
    for c in copies:
        c.start()
    for c in copies:
        c.wait()


def per_device(
    hidden_rows, key_grad, value_grad, visual_rows, visual_cotangent, norm_gain, norm_bias,
    fc1_weight, fc1_bias, fc2_weight, fc2_bias, layer_scale, token_counts, dest_offsets,
):
    anyspec = pl.BlockSpec(memory_space=pl.ANY)
    vmem = pl.BlockSpec(memory_space=pltpu.VMEM)
    dma = pltpu.SemaphoreType.DMA
    V = pltpu.VMEM
    S = pltpu.SMEM
    scratch = [
        V((512, WIDE), BF16), V((128, 512), BF16), V((256, 1024), BF16), V((4, 64, WIDE), BF16), V((4, 1024), F32),
        V((1024, 512), BF16), V((1, 512), F32), V((512, 1024), BF16), S((2, IMAGES), jnp.int32),
        V((256, 1024), BF16), V((256, 512), BF16), V((NHALF, 256, 512), F32),
        V((NHALF, NX, SPREAD, CAP, 128), BF16), V((NHALF, SPREAD, NX - 1, CAP, 128), BF16),
        V((SPREAD, CAP, 128), BF16), V((NHALF, SPREAD, CAP, 128), BF16), V((SPREAD, 3, CAP, 128), BF16),
        V((SPREAD, CAP, 128), BF16),
        V((WIDE + 80, 128), F32), V((NCORE, NY, NZ, BLK, 128), F32), V((NY, NZ, BLK, 128), F32),
        V((WIDE + 80, 256), F32), V((NCORE, N_CHIP * BLK, 256), BF16), V((N_CHIP * BLK, 256), BF16),
        V((N_CHIP * BLK, 128), F32),
        V((NY, NZ, BLK, 128), BF16), V((NY - 1, NZ, BLK, 128), BF16),
        V((NZ, BLK, 128), BF16), V((NZ - 1, BLK, 128), BF16),
        V((NZ, NY, BLK, 128), BF16), V((NY - 1, NZ, BLK, 128), BF16), V((NZ - 1, NY, BLK, 128), BF16),
        V((NZ, BLK, 128), BF16), V((NY, BLK, 128), BF16), V((NZ - 1, BLK, 128), BF16), V((NY - 1, BLK, 128), BF16),
        dma((9,)), dma((3,)), dma((3,)), dma((1,)), dma((NHALF, SPREAD)), dma((1,)), dma((SPREAD,)),
        dma((2,)), dma((2,)), dma((len(GROUPS),)), dma((len(GROUPS),)), dma((3,)), dma((3,)),
        pltpu.SemaphoreType.REGULAR((2,)),
    ]
    shapes = (
        jax.ShapeDtypeStruct((OWN, 64), F32),
        jax.ShapeDtypeStruct((OWN, 64), F32),
        jax.ShapeDtypeStruct((OWN, 128), F32),
        jax.ShapeDtypeStruct((1, SPREAD, CAP, 128), BF16),
    )
    held = (V((OWN, 64), F32), V((OWN, 64), F32), V((OWN, 128), F32), V((1, SPREAD, CAP, 128), BF16))
    results = pl.pallas_call(
        kernel,
        out_shape=held,
        in_specs=[anyspec] * 14,
        out_specs=[vmem] * 4,
        scratch_shapes=scratch,
        compiler_params=pltpu.CompilerParams(
            collective_id=0, has_side_effects=True, vmem_limit_bytes=60 * 1024 * 1024
        ),
        name="bucket",
    )(
        hidden_rows, key_grad.T, value_grad.T, visual_rows, visual_cotangent,
        norm_gain.reshape(1, -1), norm_bias.reshape(1, -1), fc1_weight, fc1_bias.reshape(1, -1),
        fc2_weight, fc2_bias.reshape(1, -1), layer_scale.reshape(1, -1), token_counts, dest_offsets,
    )
    return pl.pallas_call(
        writer,
        out_shape=shapes,
        in_specs=[vmem] * 4,
        out_specs=[anyspec] * 4,
        scratch_shapes=[dma((4,))],
        name="writer",
    )(*[pltpu.with_memory_space_constraint(r, pltpu.VMEM) for r in results])


def solution(mesh):
    placed = (
        P("dp", None), P("dp", "mp"), P("dp", "mp"), P("dp", None), P("dp", None, None, None),
        P(), P(), P(None, "mp"), P("mp"), P("mp", None), P(), P(), P("dp", None), P("dp", None),
    )
    return jax.shard_map(
        per_device,
        mesh=mesh,
        in_specs=placed,
        out_specs=(P("dp", "mp"), P("dp", "mp"), P("dp", "mp"), P("dp", None, None, "mp")),
        check_vma=False,
    )
```

time: 50.1 us -> 45.3 us (0.904)
  the two profiles are of different devices: /device:TPU:65 before, /device:TPU:4 now
where the time goes in v3:
time: 45.3 us; the launch traced here: 45.2 us
  Pallas kernels  44.5 us (98%)
  between operations  0.64 us (1%)
    pallas_call x1, Pallas kernels, per_device(): pl.pallas_call(kernel, out_shape=held, in_specs=[anyspec] * 14, out_specs...  43.9 us

profile of v3, /device:TPU:4, one launch (start us, length us, event | category | flops | bytes accessed | tf_op | source)
XLA Modules:
  0.0 45.2 jit_solution(8536356551382972001)
XLA Ops:
  0.6 43.9 %bucket.1 = (f32[38,64]{1,0:T(8,128)S(1)}, f32[38,64]{1,0:T(8,128)S(1)}, f32[38,128]{1,0:T(8,128)S(1)}, bf16[1,4,64,128]{3,2,1,0:T(8,128)(2,1)S(1)}) custom-call(bf16[512,3584]{1,0:T(8,128)(2,1)} %hid_hbm.1, bf16[64,512]{1,0:T(8,128)(2,1)} %bitcast.7, bf16[64,512]{1,0:T(8,128)(2,1)} %bitcast.8, bf16[256,1024]{1,0:T(8,128)(2,1)} %vis_hbm.1, ...), custom_call_target="tpu_custom_call" | custom-call | tf_op jit(solution)/shard_map/bucket/pallas_call | solution.py:500
  44.5 0.7 %writer.1 = (f32[38,64]{1,0:T(8,128)}, f32[38,64]{1,0:T(8,128)}, f32[38,128]{1,0:T(8,128)}, bf16[1,4,64,128]{3,2,1,0:T(8,128)(2,1)}) custom-call(f32[38,64]{1,0:T(8,128)S(1)} %get-tuple-element.8.key_i, f32[38,64]{1,0:T(8,128)S(1)} %get-tuple-element.9.val_i, f32[38,128]{1,0:T(8,128)S(1)} %get-tuple-element.10.proj_i, ...), custom_call_target="tpu_custom_call" | custom-call | tf_op jit(solution)/shard_map/writer/pallas_call | solution.py:515

commit v4 on v3

--- a/solution.py
+++ b/solution.py
@@ -20,7 +20,8 @@
 YROWS = NZ * NCORE * OWN
 WIDE = 3584
 FAR_Y = (4, 3, 5, 2, 6, 1, 7)
-CHUNK = 4
+LATE_Z = 4
+CHUNK = 2
 GROUPS = ((0, 1), (1, 2), (3, 3))
 EDGES = (0, NZ - 1)
 FAR_Z = ((5, 4, 3, 2, 1), (5, 4, 3, 0, 2), (5, 4, 0, 3, 1), (0, 1, 5, 2, 4), (0, 1, 2, 5, 3), (0, 1, 2, 3, 4))
@@ -78,29 +79,43 @@
     load(6, (kgt_hbm, kvt.at[0:64]), (vgt_hbm, kvt.at[64:128]))
 
     barrier = pltpu.get_barrier_semaphore()
-
-    def greet(dp_, mp_):
-        pl.semaphore_signal(barrier, 1, device_id=(dp_, mp_), device_id_type=MESH)
+    even = x - lax.rem(x, 2)
+    odd = even + 1
+    ring = zhi * NX
+
+    def signal(sem, dp_, mp_):
+        pl.semaphore_signal(sem, 1, device_id=(dp_, mp_), device_id_type=MESH)
 
     for d in range(1, NX):
-        greet(chip * NCORE, zhi * NX + lax.rem(x + d, NX))
+        signal(barrier, chip * NCORE, ring + lax.rem(x + d, NX))
 
     @pl.when(core == 1)
     def _():
-        greet(chip * NCORE, mp)
+        signal(barrier, chip * NCORE, mp)
 
     for d in range(1, NY):
-        greet((lax.rem(y + d, NY) * NZ + zlo) * NCORE + 1, mp)
+        signal(barrier, (lax.rem(y + d, NY) * NZ + zlo) * NCORE + 1, ring + even)
     for d in range(1, NZ):
-        greet((y * NZ + lax.rem(zlo + d, NZ)) * NCORE + 1, mp)
-    other = (1 - zhi) * NX + x
+        signal(barrier, (y * NZ + lax.rem(zlo + d, NZ)) * NCORE + 1, ring + even)
     for d in (0, 1, 2, N_CHIP - 1, N_CHIP - 2):
         there = lax.rem(chip + d, N_CHIP) * NCORE + 1
         if d:
-            greet(there, mp)
-        greet(there, other)
-    near_count = 2 * (NX - 1) + 1
-    far_count = 2 * (NY - 1 + NZ - 1 + 9)
+            signal(barrier, there, ring + even)
+        signal(barrier, there, NX - ring + odd)
+
+    def met(level, collects, count):
+        hears = (core == 1) & (x == collects)
+
+        @pl.when(hears)
+        def _():
+            pl.semaphore_wait(barrier, count)
+            signal(go.at[level], chip * NCORE, mp)
+            signal(go.at[level], chip * NCORE, ring + even + odd - x)
+            signal(go.at[level], chip * NCORE + 1, ring + even + odd - x)
+
+        @pl.when(jnp.logical_not(hears))
+        def _():
+            pl.semaphore_wait(go.at[level], 1)
 
     arrived(table, lsem.at[0])
     place = lax.broadcasted_iota(jnp.int32, (1, SLOTS), 1)
@@ -171,7 +186,7 @@
         if first == 0:
             @pl.when(core == 0)
             def _():
-                pl.semaphore_wait(barrier, near_count)
+                pl.semaphore_wait(barrier, 2 * (NX - 1) + 1)
                 pl.semaphore_signal(go.at[0], 1, device_id=partner, device_id_type=MESH)
 
             @pl.when(core == 1)
@@ -184,6 +199,28 @@
     own_cols = pl.ds(pl.multiple_of(mp * 128, 128), 128)
     for k in range(SPREAD):
         vs[k] = packed[k * CAP : (k + 1) * CAP, own_cols]
+
+    def v_copy(k):
+        return remote(vs.at[k], got.at[k, 2], got_s.at[0], got_r.at[k], (lax.rem(dp + k + 1, N_DP), mp))
+
+    def h_copy(e, k):
+        to = (lax.rem(dp + k + 1, N_DP), e * NX + x)
+        return remote(hs.at[e, k], got.at[k, zhi], got_s.at[0], got_r.at[k], to)
+
+    def send_v():
+        for k in range(SPREAD):
+            v_copy(k).start()
+
+    def own_half_in():
+        met(1, even, 4 * (NY - 1 + NZ - 1 + 4))
+
+    def other_half_in():
+        met(2, odd, 4 * 5)
+
+    @pl.when((zhi == 0) & (zlo >= LATE_Z))
+    def _():
+        own_half_in()
+        send_v()
 
     arrived(kvt, lsem.at[6])
     arrived(hid, lsem.at[7])
@@ -211,23 +248,37 @@
     kv_swap = remote(kvo.at[1 - core], kvp, swap_s.at[0], swap_r.at[0], partner)
     kv_swap.start()
 
-    def v_copy(k):
-        return remote(vs.at[k], got.at[k, 2], got_s.at[0], got_r.at[k], (lax.rem(dp + k + 1, N_DP), mp))
-
-    def h_copy(e, k):
-        to = (lax.rem(dp + k + 1, N_DP), e * NX + x)
-        return remote(hs.at[e, k], got.at[k, zhi], got_s.at[0], got_r.at[k], to)
-
     with_bias = jnp.where(zhi == 0, 1.0, 0.0)
     slot_in = lax.broadcasted_iota(jnp.int32, (CAP, 128), 0)
-    @pl.when(core == 1)
-    def _():
-        pl.semaphore_wait(barrier, far_count)
-        pl.semaphore_signal(go.at[1], 1, device_id=partner, device_id_type=MESH)
-
-    @pl.when(core == 0)
-    def _():
-        pl.semaphore_wait(go.at[1], 1)
+    def ky_copy(d):
+        to = lax.rem(y + d, NY)
+        return remote(s1k.at[to], r1k.at[d - 1], k_s.at[0], k_r.at[0], (rank_of(to, zlo), mp))
+
+    def from_z(to):
+        return lax.rem(zlo - to + NZ, NZ) - 1
+
+    def kz_copy(to):
+        return remote(s2k.at[to], r2k.at[from_z(to)], k_s.at[1], k_r.at[1], (rank_of(y, to), mp))
+
+    def send_kv():
+        kv_swap.wait()
+
+        @pl.loop(0, NY)
+        def _(yy):
+            s1k[yy] = (kvo[core, yy] + kvp[yy]).astype(BF16)
+
+        for d in FAR_Y:
+            ky_copy(d).start()
+
+    @pl.when((zhi == 0) & (zlo < LATE_Z))
+    def _():
+        own_half_in()
+        send_v()
+
+    @pl.when(zhi == 1)
+    def _():
+        own_half_in()
+        other_half_in()
 
     def sum_x(e):
         cols = pl.ds(pl.multiple_of((e * NX + x) * 128, 128), 128)
@@ -241,33 +292,13 @@
             hs[e, k] = jnp.where(slot_in < filled[k], branch, 0.0).astype(BF16)
             h_copy(e, k).start()
 
-    def send_v():
-        for k in range(SPREAD):
-            v_copy(k).start()
-
     sum_x(0)
-    pl.when(zhi == 0)(send_v)
-    def ky_copy(d):
-        to = lax.rem(y + d, NY)
-        return remote(s1k.at[to], r1k.at[d - 1], k_s.at[0], k_r.at[0], (rank_of(to, zlo), mp))
-
-    def from_z(to):
-        return lax.rem(zlo - to + NZ, NZ) - 1
-
-    def kz_copy(to):
-        return remote(s2k.at[to], r2k.at[from_z(to)], k_s.at[1], k_r.at[1], (rank_of(y, to), mp))
-
-    kv_swap.wait()
-
-    @pl.loop(0, NY)
-    def _(yy):
-        s1k[yy] = (kvo[core, yy] + kvp[yy]).astype(BF16)
-
-    for d in FAR_Y:
-        ky_copy(d).start()
-
-    sum_x(1)
-    pl.when(zhi == 1)(send_v)
+    send_kv()
+
+    @pl.when(zhi == 1)
+    def _():
+        sum_x(1)
+        send_v()
 
     arrived(cot, lsem.at[8])
 
@@ -294,6 +325,11 @@
 
     a_swap = remote(amat.at[1 - core], apar, swap_s.at[1], swap_r.at[1], partner)
     a_swap.start()
+
+    @pl.when(zhi == 0)
+    def _():
+        other_half_in()
+        sum_x(1)
 
     def hp_copy(k):
         return remote(hand.at[0, k], hpar.at[k], swap_s.at[2], swap_r.at[2], partner)
@@ -488,7 +524,7 @@
         V((NZ, BLK, 128), BF16), V((NY, BLK, 128), BF16), V((NZ - 1, BLK, 128), BF16), V((NY - 1, BLK, 128), BF16),
         dma((9,)), dma((3,)), dma((3,)), dma((1,)), dma((NHALF, SPREAD)), dma((1,)), dma((SPREAD,)),
         dma((2,)), dma((2,)), dma((len(GROUPS),)), dma((len(GROUPS),)), dma((3,)), dma((3,)),
-        pltpu.SemaphoreType.REGULAR((2,)),
+        pltpu.SemaphoreType.REGULAR((3,)),
     ]
     shapes = (
         jax.ShapeDtypeStruct((OWN, 64), F32),

time: 45.3 us -> 44.7 us (0.987)
  the two profiles are of different devices: /device:TPU:4 before, /device:TPU:1 now
where the time goes in v4:
time: 44.7 us; the launch traced here: 43.8 us
  Pallas kernels  43.1 us (96%)
  between operations  0.64 us (1%)
    pallas_call x1, Pallas kernels, per_device(): pl.pallas_call(kernel, out_shape=held, in_specs=[anyspec] * 14, out_specs...  42.4 us

profile of v4, /device:TPU:1, one launch (start us, length us, event | category | flops | bytes accessed | tf_op | source)
XLA Modules:
  0.0 43.8 jit_solution(14133828189257127017)
XLA Ops:
  0.6 42.4 %bucket.1 = (f32[38,64]{1,0:T(8,128)S(1)}, f32[38,64]{1,0:T(8,128)S(1)}, f32[38,128]{1,0:T(8,128)S(1)}, bf16[1,4,64,128]{3,2,1,0:T(8,128)(2,1)S(1)}) custom-call(bf16[512,3584]{1,0:T(8,128)(2,1)} %hid_hbm.1, bf16[64,512]{1,0:T(8,128)(2,1)} %bitcast.7, bf16[64,512]{1,0:T(8,128)(2,1)} %bitcast.8, bf16[256,1024]{1,0:T(8,128)(2,1)} %vis_hbm.1, ...), custom_call_target="tpu_custom_call" | custom-call | tf_op jit(solution)/shard_map/bucket/pallas_call | solution.py:536
  43.1 0.7 %writer.1 = (f32[38,64]{1,0:T(8,128)}, f32[38,64]{1,0:T(8,128)}, f32[38,128]{1,0:T(8,128)}, bf16[1,4,64,128]{3,2,1,0:T(8,128)(2,1)}) custom-call(f32[38,64]{1,0:T(8,128)S(1)} %get-tuple-element.8.key_i, f32[38,64]{1,0:T(8,128)S(1)} %get-tuple-element.9.val_i, f32[38,128]{1,0:T(8,128)S(1)} %get-tuple-element.10.proj_i, ...), custom_call_target="tpu_custom_call" | custom-call | tf_op jit(solution)/shard_map/writer/pallas_call | solution.py:551

commit v5 on v4

--- a/solution.py
+++ b/solution.py
@@ -22,8 +22,17 @@
 FAR_Y = (4, 3, 5, 2, 6, 1, 7)
 LATE_Z = 4
 CHUNK = 2
-GROUPS = ((0, 1), (1, 2), (3, 3))
-EDGES = (0, NZ - 1)
+Y_GROUPS = (((0, 1), (1, 1), (2, 2), (4, 2)), ((0, 1), (5, 1)))
+Z_FIRST = ((), (1, 2, 3, 4))
+SENDS = (
+    (('y', 0), ('y', 1), ('y', 2), ('y', 3)),
+    (('y', 0), ('z', 1), ('z', 2), ('z', 3), ('z', 4), ('y', 1)),
+)
+SUMS = (
+    (('kv', 0), ('sum_y', 0), ('sum_y', 1), ('sum_y', 2), ('sum_y', 3)),
+    (('sum_y', 0), ('kv', 0), ('sum_z', 0), ('sum_y', 1)),
+)
+N_GROUPS = max(len(groups) for groups in Y_GROUPS)
 FAR_Z = ((5, 4, 3, 2, 1), (5, 4, 3, 0, 2), (5, 4, 0, 3, 1), (0, 1, 5, 2, 4), (0, 1, 2, 5, 3), (0, 1, 2, 3, 4))
 
 
@@ -103,17 +112,19 @@
             signal(barrier, there, ring + even)
         signal(barrier, there, NX - ring + odd)
 
-    def met(level, collects, count):
-        hears = (core == 1) & (x == collects)
-
-        @pl.when(hears)
+    def hears(collects):
+        return (core == 1) & (x == collects)
+
+    def hear(level, collects, count):
+        @pl.when(hears(collects))
         def _():
             pl.semaphore_wait(barrier, count)
             signal(go.at[level], chip * NCORE, mp)
             signal(go.at[level], chip * NCORE, ring + even + odd - x)
             signal(go.at[level], chip * NCORE + 1, ring + even + odd - x)
 
-        @pl.when(jnp.logical_not(hears))
+    def heard(level, collects):
+        @pl.when(jnp.logical_not(hears(collects)))
         def _():
             pl.semaphore_wait(go.at[level], 1)
 
@@ -211,15 +222,16 @@
         for k in range(SPREAD):
             v_copy(k).start()
 
-    def own_half_in():
-        met(1, even, 4 * (NY - 1 + NZ - 1 + 4))
-
-    def other_half_in():
-        met(2, odd, 4 * 5)
+    own_half_in = (1, even, 4 * (NY - 1 + NZ - 1 + 4))
+    other_half_in = (2, odd, 4 * 5)
+
+    def met(level, collects, count):
+        hear(level, collects, count)
+        heard(level, collects)
 
     @pl.when((zhi == 0) & (zlo >= LATE_Z))
     def _():
-        own_half_in()
+        met(*own_half_in)
         send_v()
 
     arrived(kvt, lsem.at[6])
@@ -232,6 +244,11 @@
         kvf[cols, :] = lax.dot_general(
             hid[:, cols], kv, (((0,), (0,)), ((), ())), preferred_element_type=F32
         )
+
+    @pl.when(zhi == 1)
+    def _():
+        hear(*own_half_in)
+        hear(*other_half_in)
 
     colsum = jnp.sum(kv.astype(F32), axis=0, keepdims=True)
     tail_row = lax.broadcasted_iota(jnp.int32, (80, 128), 0)
@@ -272,13 +289,13 @@
 
     @pl.when((zhi == 0) & (zlo < LATE_Z))
     def _():
-        own_half_in()
+        met(*own_half_in)
         send_v()
 
     @pl.when(zhi == 1)
     def _():
-        own_half_in()
-        other_half_in()
+        heard(1, even)
+        heard(2, odd)
 
     def sum_x(e):
         cols = pl.ds(pl.multiple_of((e * NX + x) * 128, 128), 128)
@@ -328,7 +345,7 @@
 
     @pl.when(zhi == 0)
     def _():
-        other_half_in()
+        met(*other_half_in)
         sum_x(1)
 
     def hp_copy(k):
@@ -369,41 +386,27 @@
         res = half[rows, :] + jnp.dot(apar[rows, :], theirs, preferred_element_type=F32)
         s1p[z] = res.astype(BF16).reshape(NY, BLK, 128)
 
-    inner = (zlo > 0) & (zlo < NZ - 1)
-    z_first = (core == 1) & inner
-
-    @pl.when(core == 0)
-    def _():
-        for i, (first, count) in enumerate(GROUPS):
-            for z in range(first, first + count):
-                block_rows(z)
-            for d in FAR_Y:
-                p1y_copy(d, i, first, count).start()
-
-    @pl.when(core == 1)
-    def _():
-        for i, z in enumerate(EDGES):
+    def kv_sum():
+        total = s1k[y].astype(F32)
+        arrived(r1k, k_r.at[0])
+        for d in range(1, NY):
+            total = total + r1k[d - 1].astype(F32)
+        s2k[...] = total.astype(BF16)
+        for to in far:
+            kz_copy(to).start()
+
+    def send_y(i, first, count):
+        for z in range(first, first + count):
             block_rows(z)
-            for d in FAR_Y:
-                p1y_copy(d, i, z, 1).start()
-            if i == 0:
-                for to in far:
-                    @pl.when((to > 0) & (to < NZ - 1))
-                    def _():
-                        block_rows(to)
-                        p1z_copy(to).start()
-
-                @pl.when(inner)
-                def _():
-                    block_rows(zlo)
-
-    total = s1k[y].astype(F32)
-    arrived(r1k, k_r.at[0])
-    for d in range(1, NY):
-        total = total + r1k[d - 1].astype(F32)
-    s2k[...] = total.astype(BF16)
-    for to in far:
-        kz_copy(to).start()
+        for d in FAR_Y:
+            p1y_copy(d, i, first, count).start()
+
+    def send_z(z):
+        block_rows(z)
+
+        @pl.when(zlo != z)
+        def _():
+            p1z_copy(z).start()
 
     def sum_y(i, first, count):
         total = s1p[first : first + count, y].astype(F32)
@@ -416,16 +419,14 @@
             def _():
                 p2z_copy(z).start()
 
-    @pl.when(core == 0)
-    def _():
-        for i, (first, count) in enumerate(GROUPS):
-            sum_y(i, first, count)
-
-    @pl.when(core == 1)
-    def _():
-        sum_y(0, EDGES[0], 1)
-
-        @pl.when(inner)
+    def one_of(zs):
+        hit = zlo == zs[0]
+        for z in zs[1:]:
+            hit = hit | (zlo == z)
+        return hit
+
+    def sum_z(zs):
+        @pl.when(one_of(zs))
         def _():
             total = s1p[zlo].astype(F32)
             arrived(r1z, p_r.at[0])
@@ -435,7 +436,27 @@
             for d in FAR_Y:
                 p2y_copy(d).start()
 
-        sum_y(1, EDGES[1], 1)
+    def follow(c, steps):
+        groups, zs = Y_GROUPS[c], Z_FIRST[c]
+
+        @pl.when(core == c)
+        def _():
+            for kind, i in steps:
+                if kind == "kv":
+                    kv_sum()
+                elif kind == "sum_y":
+                    sum_y(i, *groups[i])
+                elif kind == "sum_z":
+                    sum_z(zs)
+                elif kind == "y":
+                    send_y(i, *groups[i])
+                else:
+                    send_z(i)
+
+    for c in range(NCORE):
+        follow(c, SENDS[c])
+    for c in range(NCORE):
+        follow(c, SUMS[c])
 
     total = s2k[zlo].astype(F32)
     arrived(r2k, k_r.at[1])
@@ -451,26 +472,34 @@
     arrived(r1k, k_s.at[0])
     arrived(r2k, k_s.at[1])
 
-    @pl.when(core == 0)
-    def _():
-        for i, (first, count) in enumerate(GROUPS):
-            arrived(r1y.at[:, pl.ds(first, count)], p1y_s.at[i])
-        arrived(r2z, p_s.at[1])
-
-    @pl.when(core == 1)
-    def _():
-        for i, z in enumerate(EDGES):
-            arrived(r1y.at[:, pl.ds(z, 1)], p1y_s.at[i])
-
-        @pl.when(inner)
+    for c in range(NCORE):
+        @pl.when(core == c)
         def _():
-            arrived(r1z.at[0 : NZ - 3], p_s.at[0])
-            arrived(s2z.at[0:2], p_s.at[1])
-
-        @pl.when(jnp.logical_not(inner))
-        def _():
-            arrived(r1z.at[0 : NZ - 2], p_s.at[0])
-            arrived(s2z.at[0:1], p_s.at[1])
+            zs = Z_FIRST[c]
+            for i, (first, count) in enumerate(Y_GROUPS[c]):
+                arrived(r1y.at[:, pl.ds(first, count)], p1y_s.at[i])
+            if not zs:
+                arrived(r2z, p_s.at[1])
+                return
+            mine = one_of(zs)
+
+            @pl.when(mine)
+            def _():
+                if len(zs) > 1:
+                    arrived(r1z.at[0 : len(zs) - 1], p_s.at[0])
+                if len(zs) < NZ:
+                    arrived(s2z.at[0 : NZ - len(zs)], p_s.at[1])
+
+            @pl.when(jnp.logical_not(mine))
+            def _():
+                arrived(r1z.at[0 : len(zs)], p_s.at[0])
+                if len(zs) < NZ - 1:
+                    arrived(s2z.at[0 : NZ - len(zs) - 1], p_s.at[1])
+
+    z_first = jnp.bool_(False)
+    for c in range(NCORE):
+        if Z_FIRST[c]:
+            z_first = z_first | ((core == c) & one_of(Z_FIRST[c]))
 
     @pl.when(z_first)
     def _():
@@ -523,7 +552,7 @@
         V((NZ, NY, BLK, 128), BF16), V((NY - 1, NZ, BLK, 128), BF16), V((NZ - 1, NY, BLK, 128), BF16),
         V((NZ, BLK, 128), BF16), V((NY, BLK, 128), BF16), V((NZ - 1, BLK, 128), BF16), V((NY - 1, BLK, 128), BF16),
         dma((9,)), dma((3,)), dma((3,)), dma((1,)), dma((NHALF, SPREAD)), dma((1,)), dma((SPREAD,)),
-        dma((2,)), dma((2,)), dma((len(GROUPS),)), dma((len(GROUPS),)), dma((3,)), dma((3,)),
+        dma((2,)), dma((2,)), dma((N_GROUPS,)), dma((N_GROUPS,)), dma((3,)), dma((3,)),
         pltpu.SemaphoreType.REGULAR((3,)),
     ]
     shapes = (

time: 44.7 us -> 44 us (0.984)
  no operation moved by 1% of the time
where the time goes in v5:
time: 44 us; the launch traced here: 43.5 us
  Pallas kernels  42.9 us (98%)
  between operations  0.64 us (1%)
    pallas_call x1, Pallas kernels, per_device(): pl.pallas_call(kernel, out_shape=held, in_specs=[anyspec] * 14, out_specs...  42.2 us

profile of v5, /device:TPU:1, one launch (start us, length us, event | category | flops | bytes accessed | tf_op | source)
XLA Modules:
  0.0 43.5 jit_solution(4850594029167993722)
XLA Ops:
  0.6 42.2 %bucket.1 = (f32[38,64]{1,0:T(8,128)S(1)}, f32[38,64]{1,0:T(8,128)S(1)}, f32[38,128]{1,0:T(8,128)S(1)}, bf16[1,4,64,128]{3,2,1,0:T(8,128)(2,1)S(1)}) custom-call(bf16[512,3584]{1,0:T(8,128)(2,1)} %hid_hbm.1, bf16[64,512]{1,0:T(8,128)(2,1)} %bitcast.7, bf16[64,512]{1,0:T(8,128)(2,1)} %bitcast.8, bf16[256,1024]{1,0:T(8,128)(2,1)} %vis_hbm.1, ...), custom_call_target="tpu_custom_call" | custom-call | tf_op jit(solution)/shard_map/bucket/pallas_call | solution.py:565
  42.8 0.7 %writer.1 = (f32[38,64]{1,0:T(8,128)}, f32[38,64]{1,0:T(8,128)}, f32[38,128]{1,0:T(8,128)}, bf16[1,4,64,128]{3,2,1,0:T(8,128)(2,1)}) custom-call(f32[38,64]{1,0:T(8,128)S(1)} %get-tuple-element.8.key_i, f32[38,64]{1,0:T(8,128)S(1)} %get-tuple-element.9.val_i, f32[38,128]{1,0:T(8,128)S(1)} %get-tuple-element.10.proj_i, ...), custom_call_target="tpu_custom_call" | custom-call | tf_op jit(solution)/shard_map/writer/pallas_call | solution.py:580

commit v6 on v5

--- a/solution.py
+++ b/solution.py
@@ -21,12 +21,13 @@
 WIDE = 3584
 FAR_Y = (4, 3, 5, 2, 6, 1, 7)
 LATE_Z = 4
+NORM_ROWS = 32
 CHUNK = 2
 Y_GROUPS = (((0, 1), (1, 1), (2, 2), (4, 2)), ((0, 1), (5, 1)))
 Z_FIRST = ((), (1, 2, 3, 4))
 SENDS = (
     (('y', 0), ('y', 1), ('y', 2), ('y', 3)),
-    (('y', 0), ('z', 1), ('z', 2), ('z', 3), ('z', 4), ('y', 1)),
+    (('y', 0), ('z', 1), ('z', 2), ('z', 3), ('y', 1), ('z', 4)),
 )
 SUMS = (
     (('kv', 0), ('sum_y', 0), ('sum_y', 1), ('sum_y', 2), ('sum_y', 3)),
@@ -41,7 +42,7 @@
     cnt_hbm, off_hbm,
     keyv, valv, projv, hand,
     hid, kvt, vis, cot, vecs, w1, b1, w2, table,
-    packed, hidden, part, xs, xr, vs, hs, got, hpar,
+    packed, normed, hidden, part, xs, xr, vs, hs, got, hpar,
     kvf, kvo, kvp, cotf, amat, apar, half,
     s1k, r1k, s2k, r2k, s1p, r1y, r1z, s2z, s2y, r2z, r2y,
     lsem, swap_s, swap_r, x_s, x_r, got_s, got_r, k_s, k_r, p1y_s, p1y_r, p_s, p_r, go,
@@ -155,7 +156,7 @@
     def x_copy(e, d, k):
         to = lax.rem(x + d, NX)
         return remote(
-            xs.at[e, to, k], xr.at[e, k, d - 1], x_s.at[0], x_r.at[e, k], (dp, zhi * NX + to)
+            xs.at[e, to, k], xr.at[e, k, d - 1], x_s.at[0], x_r.at[SPREAD if e else k], (dp, zhi * NX + to)
         )
 
     def second(e, first, count):
@@ -174,21 +175,22 @@
                 x_copy(e, d, k).start()
 
     arrived(vis, lsem.at[1])
+    packed[...] = jnp.dot(select, vis[...], preferred_element_type=F32).astype(BF16)
+    arrived(vecs, lsem.at[2])
+    for at in range(0, SLOTS, NORM_ROWS):
+        some = slice(at, at + NORM_ROWS)
+        values = packed[some].astype(F32)
+        center = jnp.mean(values, axis=1, keepdims=True)
+        delta = values - center
+        spread_sq = jnp.mean(delta * delta, axis=1, keepdims=True)
+        normed[some] = (delta * lax.rsqrt(spread_sq + 1e-06) * vecs[0:1, :] + vecs[1:2, :]).astype(BF16)
     for first in range(0, SPREAD, CHUNK):
         rows = slice(first * CAP, (first + CHUNK) * CAP)
-        placed = jnp.dot(select[rows], vis[...], preferred_element_type=F32)
-        packed[rows] = placed.astype(BF16)
-        center = jnp.mean(placed, axis=1, keepdims=True)
-        delta = placed - center
-        spread_sq = jnp.mean(delta * delta, axis=1, keepdims=True)
-        if first == 0:
-            arrived(vecs, lsem.at[2])
-        normed = (delta * lax.rsqrt(spread_sq + 1e-06) * vecs[0:1, :] + vecs[1:2, :]).astype(BF16)
         if first == 0:
             arrived(w1, lsem.at[3])
             arrived(b1, lsem.at[4])
             load(7, (hid_hbm, hid))
-        pre = jnp.dot(normed, w1[...], preferred_element_type=F32) + b1[...]
+        pre = jnp.dot(normed[rows], w1[...], preferred_element_type=F32) + b1[...]
         hidden[rows] = (0.5 * pre * (1.0 + lax.erf(pre * (0.5**0.5)))).astype(BF16)
         if first == 0:
             arrived(w2, lsem.at[5])
@@ -300,8 +302,11 @@
     def sum_x(e):
         cols = pl.ds(pl.multiple_of((e * NX + x) * 128, 128), 128)
         own = pl.ds(pl.multiple_of(x * 128, 128), 128)
+        if e:
+            arrived(xr.at[e], x_r.at[SPREAD])
         for k in range(SPREAD):
-            arrived(xr.at[e, k], x_r.at[e, k])
+            if not e:
+                arrived(xr.at[e, k], x_r.at[k])
             total = part[e, k * CAP : (k + 1) * CAP, own]
             for d in range(1, NX):
                 total = total + xr[e, k, d - 1].astype(F32)
@@ -368,7 +373,7 @@
         to = lax.rem(y + d, NY)
         zs = pl.ds(first, count)
         return remote(
-            s1p.at[zs, to], r1y.at[d - 1, zs], p1y_s.at[i], p1y_r.at[i], (rank_of(to, zlo), mp)
+            s1p.at[zs, to], r1y.at[d - 1, zs], p1y_s.at[0], p1y_r.at[i], (rank_of(to, zlo), mp)
         )
 
     def p1z_copy(to):
@@ -476,8 +481,7 @@
         @pl.when(core == c)
         def _():
             zs = Z_FIRST[c]
-            for i, (first, count) in enumerate(Y_GROUPS[c]):
-                arrived(r1y.at[:, pl.ds(first, count)], p1y_s.at[i])
+            arrived(r1y.at[:, pl.ds(0, NZ - len(zs))], p1y_s.at[0])
             if not zs:
                 arrived(r2z, p_s.at[1])
                 return
@@ -540,7 +544,7 @@
     scratch = [
         V((512, WIDE), BF16), V((128, 512), BF16), V((256, 1024), BF16), V((4, 64, WIDE), BF16), V((4, 1024), F32),
         V((1024, 512), BF16), V((1, 512), F32), V((512, 1024), BF16), S((2, IMAGES), jnp.int32),
-        V((256, 1024), BF16), V((256, 512), BF16), V((NHALF, 256, 512), F32),
+        V((256, 1024), BF16), V((256, 1024), BF16), V((256, 512), BF16), V((NHALF, 256, 512), F32),
         V((NHALF, NX, SPREAD, CAP, 128), BF16), V((NHALF, SPREAD, NX - 1, CAP, 128), BF16),
         V((SPREAD, CAP, 128), BF16), V((NHALF, SPREAD, CAP, 128), BF16), V((SPREAD, 3, CAP, 128), BF16),
         V((SPREAD, CAP, 128), BF16),
@@ -551,8 +555,8 @@
         V((NZ, BLK, 128), BF16), V((NZ - 1, BLK, 128), BF16),
         V((NZ, NY, BLK, 128), BF16), V((NY - 1, NZ, BLK, 128), BF16), V((NZ - 1, NY, BLK, 128), BF16),
         V((NZ, BLK, 128), BF16), V((NY, BLK, 128), BF16), V((NZ - 1, BLK, 128), BF16), V((NY - 1, BLK, 128), BF16),
-        dma((9,)), dma((3,)), dma((3,)), dma((1,)), dma((NHALF, SPREAD)), dma((1,)), dma((SPREAD,)),
-        dma((2,)), dma((2,)), dma((N_GROUPS,)), dma((N_GROUPS,)), dma((3,)), dma((3,)),
+        dma((9,)), dma((3,)), dma((3,)), dma((1,)), dma((SPREAD + 1,)), dma((1,)), dma((SPREAD,)),
+        dma((2,)), dma((2,)), dma((1,)), dma((N_GROUPS,)), dma((3,)), dma((3,)),
         pltpu.SemaphoreType.REGULAR((3,)),
     ]
     shapes = (

time: 44 us -> 43.9 us (level)
  no operation moved by 1% of the time
where the time goes in v6:
time: 43.9 us; the launch traced here: 43.1 us
  Pallas kernels  42.5 us (97%)
  between operations  0.64 us (1%)
    pallas_call x1, Pallas kernels, per_device(): pl.pallas_call(kernel, out_shape=held, in_specs=[anyspec] * 14, out_specs...  41.8 us

profile of v6, /device:TPU:1, one launch (start us, length us, event | category | flops | bytes accessed | tf_op | source)
XLA Modules:
  0.0 43.1 jit_solution(1900931457908133421)
XLA Ops:
  0.6 41.8 %bucket.1 = (f32[38,64]{1,0:T(8,128)S(1)}, f32[38,64]{1,0:T(8,128)S(1)}, f32[38,128]{1,0:T(8,128)S(1)}, bf16[1,4,64,128]{3,2,1,0:T(8,128)(2,1)S(1)}) custom-call(bf16[512,3584]{1,0:T(8,128)(2,1)} %hid_hbm.1, bf16[64,512]{1,0:T(8,128)(2,1)} %bitcast.7, bf16[64,512]{1,0:T(8,128)(2,1)} %bitcast.8, bf16[256,1024]{1,0:T(8,128)(2,1)} %vis_hbm.1, ...), custom_call_target="tpu_custom_call" | custom-call | tf_op jit(solution)/shard_map/bucket/pallas_call | solution.py:569
  42.5 0.7 %writer.1 = (f32[38,64]{1,0:T(8,128)}, f32[38,64]{1,0:T(8,128)}, f32[38,128]{1,0:T(8,128)}, bf16[1,4,64,128]{3,2,1,0:T(8,128)(2,1)}) custom-call(f32[38,64]{1,0:T(8,128)S(1)} %get-tuple-element.8.key_i, f32[38,64]{1,0:T(8,128)S(1)} %get-tuple-element.9.val_i, f32[38,128]{1,0:T(8,128)S(1)} %get-tuple-element.10.proj_i, ...), custom_call_target="tpu_custom_call" | custom-call | tf_op jit(solution)/shard_map/writer/pallas_call | solution.py:584

commit v7 on v6

--- a/solution.py
+++ b/solution.py
@@ -171,7 +171,7 @@
 
     def send_x(e, first, count):
         for k in range(first, first + count):
-            for d in (2, 1, 3):
+            for d in (1, 3, 2):
                 x_copy(e, d, k).start()
 
     arrived(vis, lsem.at[1])

time: 43.9 us -> 43.9 us (level)
  no operation moved by 1% of the time
where the time goes in v7:
time: 43.9 us; the launch traced here: 43 us
  Pallas kernels  42.4 us (97%)
  between operations  0.64 us (1%)
    pallas_call x1, Pallas kernels, per_device(): pl.pallas_call(kernel, out_shape=held, in_specs=[anyspec] * 14, out_specs...  41.7 us

profile of v7, /device:TPU:1, one launch (start us, length us, event | category | flops | bytes accessed | tf_op | source)
XLA Modules:
  0.0 43.0 jit_solution(545293537803693692)
XLA Ops:
  0.6 41.7 %bucket.1 = (f32[38,64]{1,0:T(8,128)S(1)}, f32[38,64]{1,0:T(8,128)S(1)}, f32[38,128]{1,0:T(8,128)S(1)}, bf16[1,4,64,128]{3,2,1,0:T(8,128)(2,1)S(1)}) custom-call(bf16[512,3584]{1,0:T(8,128)(2,1)} %hid_hbm.1, bf16[64,512]{1,0:T(8,128)(2,1)} %bitcast.7, bf16[64,512]{1,0:T(8,128)(2,1)} %bitcast.8, bf16[256,1024]{1,0:T(8,128)(2,1)} %vis_hbm.1, ...), custom_call_target="tpu_custom_call" | custom-call | tf_op jit(solution)/shard_map/bucket/pallas_call | solution.py:569
  42.3 0.7 %writer.1 = (f32[38,64]{1,0:T(8,128)}, f32[38,64]{1,0:T(8,128)}, f32[38,128]{1,0:T(8,128)}, bf16[1,4,64,128]{3,2,1,0:T(8,128)(2,1)}) custom-call(f32[38,64]{1,0:T(8,128)S(1)} %get-tuple-element.8.key_i, f32[38,64]{1,0:T(8,128)S(1)} %get-tuple-element.9.val_i, f32[38,128]{1,0:T(8,128)S(1)} %get-tuple-element.10.proj_i, ...), custom_call_target="tpu_custom_call" | custom-call | tf_op jit(solution)/shard_map/writer/pallas_call | solution.py:584
